TPU v7x, 32 devices: a whole 2x2x4 slice. The times are simulated.
32 devices in a mesh: obs: 8 (over z, x), bel: 4 (over y, core).
Axes of the slice: x: 2, y: 2, z: 4, core: 2. Of those that a mesh axis runs over, the one named last changes fastest.
Arguments:
- alpha_set: bfloat16 [2048, 2048], P('bel'), may hold values from -600 to 600
- transitions: bfloat16 [16, 2048, 2048], P(None, 'obs'), may hold values from 0.0009994507 to 1
- obs_weights: float32 [256, 16, 2048], P('obs'), may hold values from 0.01 to 1
- rewards: float32 [16, 2048], replicated, may hold values from -1 to 1
- chosen_idx: int32 [1536, 16, 256], P('bel', None, 'obs'), may hold values from 0 to 2047
- chosen_action: int32 [1536], P('bel'), may hold values from 0 to 15
Outputs:
- new_alpha: float32 [1536, 2048], P(('bel', 'obs'))
Inputs may be any that keep to these rules, and one draw needn't show every extreme that they name: `chosen_idx`: an index into the 2048 alpha vectors. `chosen_action`: an index into the 16 actions.
All inputs are finite; a program needn't handle non-finite values.
Results may differ from a plain program's by a relative error of at most 0.0003.
Values may be sent and summed in bfloat16 or wider, within the bound.
A program may use at most 192 MiB of HBM per device.

v0:
```python
import functools

import jax
import jax.numpy as jnp
from jax import lax
from jax.experimental import pallas as pl
from jax.experimental.pallas import tpu as pltpu
from jax.sharding import PartitionSpec as P

discount = 0.95
lanes = 128


def gather_kernel(picks_ref, act_ref, alpha_ref, weights_ref, moves_ref, out_ref):
    beliefs = act_ref.shape[0]
    obs_local = picks_ref.shape[0] // beliefs
    actions = weights_ref.shape[0] // obs_local
    slabs = alpha_ref.shape[1]
    rows = out_ref.shape[0] // slabs

    def one(b, carry):
        action = act_ref[b]
        sums = [None] * min(4, obs_local)
        for o in range(obs_local):
            row = alpha_ref[picks_ref[b * obs_local + o]].astype(jnp.float32)
            term = row * weights_ref[o * actions + action]
            at = o % len(sums)
            sums[at] = term if sums[at] is None else sums[at] + term
        out_ref[pl.ds(b, slabs, stride=rows), :] = functools.reduce(jnp.add, sums)
        return carry

    lax.fori_loop(0, beliefs, one, 0)

    def total(a, carry):
        acc = weights_ref[a]
        for o in range(1, obs_local):
            acc = acc + weights_ref[o * actions + a]
        out_ref[pl.ds(beliefs + a, slabs, stride=rows), :] = acc
        out_ref[pl.ds(beliefs + actions + a, slabs, stride=rows), :] = moves_ref[a]
        return carry

    lax.fori_loop(0, actions, total, 0)


def gather_rows(picks, acts, alpha, weights, moves):
    slabs = alpha.shape[1]
    beliefs = acts.shape[0]
    rows = beliefs + 2 * moves.shape[0]
    vmem = pl.BlockSpec(memory_space=pltpu.VMEM)
    smem = pl.BlockSpec(memory_space=pltpu.SMEM)
    out = pl.pallas_call(
        gather_kernel,
        out_shape=jax.ShapeDtypeStruct((slabs * rows, lanes), jnp.float32),
        in_specs=[smem, smem, vmem, vmem, vmem],
        out_specs=vmem,
        compiler_params=pltpu.CompilerParams(vmem_limit_bytes=40 << 20),
        cost_estimate=pl.CostEstimate(
            flops=80_000_000, bytes_accessed=16 << 20, transcendentals=0
        ),
        name="gather_rows",
    )(picks, acts, alpha, weights, moves)
    return out.reshape(slabs, rows, lanes)


def move_kernel(act_ref, w_ref, tot_ref, table_ref, out_ref):
    a = pl.program_id(0)
    scaled = w_ref[...] / tot_ref[0]
    x = jnp.where(act_ref[...] == a, scaled, 0.0)
    high = x.astype(jnp.bfloat16)
    low = (x - high.astype(jnp.float32)).astype(jnp.bfloat16)
    table = table_ref[0]
    both = jnp.dot(jnp.concatenate([high, low], axis=0), table, preferred_element_type=jnp.float32)
    half = x.shape[0]
    part = both[:half] + both[half:]

    @pl.when(a == 0)
    def _():
        out_ref[...] = part

    @pl.when(a > 0)
    def _():
        out_ref[...] += part


def move(acts, weighted, totals, table):
    beliefs, width = weighted.shape
    actions, _, states = table.shape
    return pl.pallas_call(
        move_kernel,
        grid=(actions,),
        out_shape=jax.ShapeDtypeStruct((beliefs, states), jnp.float32),
        in_specs=[
            pl.BlockSpec((beliefs, 1), lambda a: (0, 0)),
            pl.BlockSpec((beliefs, width), lambda a: (0, 0)),
            pl.BlockSpec((1, 1, width), lambda a: (a, 0, 0)),
            pl.BlockSpec((1, width, states), lambda a: (a, 0, 0)),
        ],
        out_specs=pl.BlockSpec((beliefs, states), lambda a: (0, 0)),
        compiler_params=pltpu.CompilerParams(
            vmem_limit_bytes=48 << 20, dimension_semantics=("arbitrary",)
        ),
        cost_estimate=pl.CostEstimate(
            flops=4 * beliefs * width * actions * states,
            bytes_accessed=2 * actions * width * states,
            transcendentals=0,
        ),
        name="move",
    )(acts[:, None], weighted, totals[:, None, :], table)


def action_table(actions, count):
    return (actions[:, None] == jnp.arange(count, dtype=jnp.int32)[None, :]).astype(jnp.float32)


def body(alpha_set, transitions, obs_weights, rewards, chosen_idx, chosen_action):
    actions, states = rewards.shape
    obs_local = obs_weights.shape[0]
    beliefs = chosen_action.shape[0]
    slabs = states // lanes
    ranks = lax.axis_size("obs")
    action_hot = action_table(chosen_action, actions)
    picks = jnp.sum(jnp.where(action_hot[:, :, None] > 0, chosen_idx, 0), axis=1).reshape(-1)
    alpha = lax.all_gather(alpha_set.reshape(-1, slabs, lanes), "bel", axis=0, tiled=True)
    weights = obs_weights.reshape(obs_local * actions, slabs, lanes)
    trans_part = jnp.sum(transitions.astype(jnp.float32), axis=1).reshape(actions, slabs, lanes)
    partial = gather_rows(picks, chosen_action, alpha, weights, trans_part)
    rows = partial.shape[1]
    if slabs % ranks == 0:
        piece = lax.psum_scatter(partial, "obs", scatter_dimension=0, tiled=True)
        piece = piece.transpose(1, 0, 2).reshape(rows, -1)
    else:
        flat = partial.transpose(1, 0, 2).reshape(rows, states)
        piece = lax.psum_scatter(flat, "obs", scatter_dimension=1, tiled=True)
    trans_totals = lax.all_gather(piece[beliefs + actions :], "obs", axis=1, tiled=True)
    moved = move(
        chosen_action, piece[:beliefs], piece[beliefs : beliefs + actions], transitions
    )
    future = lax.psum_scatter(moved, "obs", scatter_dimension=0, tiled=True)
    owned = beliefs // ranks
    own_hot = lax.dynamic_slice_in_dim(action_hot, lax.axis_index("obs") * owned, owned, 0)
    own = functools.partial(
        jnp.dot, own_hot, precision=lax.Precision.HIGHEST, preferred_element_type=jnp.float32
    )
    return own(rewards) + discount * (future / own(trans_totals))


def solution(mesh):
    placed = (
        P("bel", None),
        P(None, "obs", None),
        P("obs", None, None),
        P(),
        P("bel", None, "obs"),
        P("bel"),
    )
    return jax.shard_map(
        body, mesh=mesh, in_specs=placed, out_specs=P(("bel", "obs"), None), check_vma=False
    )
```

profile of v0, /device:TPU:0, one launch (start us, length us, event | category | flops | bytes accessed | tf_op | source)
XLA Modules:
  0.0 285.7 jit_solution(14449361546637342965)
XLA Ops:
  6.5 0.0 copy-start
  6.5 0.0 copy-start.2
  6.5 0.0 copy-start.3
  6.5 0.0 all-gather.2.cloned.1.call-start
  6.5 3.6 %copy.21 = bf16[64,8,16,128]{3,2,1,0:T(8,128)(2,1)} copy(bf16[64,8,16,128]{3,1,2,0:T(8,128)(2,1)} %bitcast.27) | data formatting | bytes 4194304
  10.2 0.0 all-gather.2.cloned.1.call-update
  10.2 0.0 reduce-scatter.3.cloned.1.call-start
  10.3 0.0 copy-done.2
  10.3 0.0 copy-done.3
  10.3 0.1 select_reduce_fusion
  10.4 0.1 copy.14
  10.5 0.1 reshape.43.picks_ref
  10.6 5.1 %copy.22 = f32[64,8,16,128]{3,2,1,0:T(8,128)} copy(f32[64,8,16,128]{3,1,2,0:T(8,128)} %bitcast.26) | data formatting | bytes 8388608
  15.7 8.0 %convert_reduce_fusion = f32[16,2048]{1,0:T(8,128)S(1)} fusion(bf16[16,256,2048]{2,1,0:T(8,128)(2,1)} %table_ref.1), kind=kLoop, calls=%fused_computation | loop fusion | flops 16744448 | bytes 16908288 | tf_op jit(solution)/shard_map/reduce_sum | solution.py:125
  23.7 47.7 %all-gather.2.cloned.1.call-done.alpha_ref = bf16[2048,16,128]{2,1,0:T(8,128)(2,1)} async-done(((bf16[512,16,128]{2,1,0:T(8,128)(2,1)}), bf16[2048,16,128]{2,1,0:T(8,128)(2,1)}) %all-gather.2.cloned.1.call-update) | async-done | bytes 8388624 | tf_op jit(solution)/shard_map/all_gather | solution.py:123
  71.3 0.0 copy-start.1
  71.3 2.2 copy-done.1
  73.5 23.5 %gather_rows.1 = f32[6656,128]{1,0:T(8,128)} custom-call(s32[12288]{0:T(1024)S(1)} %reshape.43.picks_ref, s32[384]{0:T(512)S(1)} %copy-done.2, bf16[2048,16,128]{2,1,0:T(8,128)(2,1)} %all-gather.2.cloned.1.call-done.alpha_ref, f32[512,16,128]{2,1,0:T(8,128)S(1)} %bitcast.22, f32[16,16,128]{2,1,0:T(8,128)S(1)} %bitcast.23), custom_call_target="tpu_custom_call" | custom-call | flops 80000000 | bytes 16777216 | tf_op jit(solution)/shard_map/gather_rows/pallas_call | solution.py:51
  97.1 0.0 reduce-scatter.3.cloned.1.call-update
  97.1 0.0 reduce-scatter.5.cloned.1.call-start
  97.1 0.1 broadcast_in_dim.25.act_ref
  97.3 77.9 %reduce-scatter.3.cloned.1.call-done = f32[2,416,128]{2,1,0:T(8,128)} async-done(((f32[16,416,128]{2,1,0:T(8,128)}), f32[2,416,128]{2,1,0:T(8,128)}) %reduce-scatter.3.cloned.1.call-update) | async-done | bytes 426000 | tf_op jit(solution)/shard_map/reduce_scatter | solution.py:129
  175.1 0.7 slice_bitcast_fusion.1
  175.9 1.0 copy_bitcast_fusion.w_ref
  176.9 24.6 %move.1 = f32[384,2048]{1,0:T(8,128)} custom-call(s32[384,1]{1,0:T(8,128)S(1)} %broadcast_in_dim.25.act_ref, f32[384,256]{1,0:T(8,128)S(1)} %copy_bitcast_fusion.w_ref, f32[16,1,256]{2,1,0:T(1,128)S(1)} %bitcast.24, bf16[16,256,2048]{2,1,0:T(8,128)(2,1)} %table_ref.1), custom_call_target="tpu_custom_call" | custom-call | flops 12884901888 | bytes 16777216 | tf_op jit(solution)/shard_map/move/pallas_call | solution.py:88
  201.5 0.0 reduce-scatter.5.cloned.1.call-update
  201.5 31.3 %all_gather.7 = f32[16,2048]{1,0:T(8,128)S(1)} all-gather(f32[16,256]{1,0:T(8,128)S(1)} %bitcast.31), channel_id=1, replica_groups=mesh['obs'=8,'bel'=4] {'obs'}, dimensions={1}, use_global_device_ids=true | all-gather | bytes 147456 | tf_op jit(solution)/shard_map/all_gather | solution.py:134
  232.8 43.7 %reduce-scatter.5.cloned.1.call-done = f32[48,2048]{1,0:T(8,128)} async-done(((f32[384,2048]{1,0:T(8,128)}), f32[48,2048]{1,0:T(8,128)}) %reduce-scatter.5.cloned.1.call-update) | async-done | bytes 393232 | tf_op jit(solution)/shard_map/reduce_scatter | solution.py:138
  276.5 1.4 fusion
  277.9 0.0 copy-done
  277.9 1.2 convolution_add_fusion
  (4 shorter events, 0.1 us)
Async XLA Ops:
  6.5 271.4 %copy-start = (f32[16,2048]{1,0:T(8,128)S(1)}, f32[16,2048]{1,0:T(8,128)}, u32[]{:S(2)}) copy-start(f32[16,2048]{1,0:T(8,128)} %param.9) | copy-start | bytes 393220
  6.5 3.7 %copy-start.2 = (s32[384]{0:T(512)S(1)}, s32[384]{0:T(512)}, u32[]{:S(2)}) copy-start(s32[384]{0:T(512)} %act_ref.1) | copy-start | bytes 4612
  6.5 3.7 %copy-start.3 = (s32[384,16,32]{0,2,1:T(8,128)S(1)}, s32[384,16,32]{0,2,1:T(8,128)}, u32[]{:S(2)}) copy-start(s32[384,16,32]{0,2,1:T(8,128)} %param.10) | copy-start | bytes 2359300
  6.5 64.8 %all-gather.2.cloned.1.call-start = ((), (), s32[]{:S(2)}) async-start(), calls=%async_computation.2 | async-start | bytes 10485760 | tf_op jit(solution)/shard_map/all_gather | solution.py:123
  10.2 164.9 %reduce-scatter.3.cloned.1.call-start = ((), (), s32[]{:S(2)}) async-start(), calls=%async_computation.3 | async-start | bytes 3833856 | tf_op jit(solution)/shard_map/reduce_scatter | solution.py:129
  71.3 2.2 copy-start.1
  97.1 179.4 %reduce-scatter.5.cloned.1.call-start = ((), (), s32[]{:S(2)}) async-start(), calls=%async_computation.4 | async-start | bytes 3538944 | tf_op jit(solution)/shard_map/reduce_scatter | solution.py:138
Sparse Core Ops, SparseCore 0:
  10.3 60.9 all-gather.1
  97.2 77.8 reduce-scatter.2
  201.6 74.8 reduce-scatter.4
where the time goes:
time: 286 us
  waiting for transfers between devices  169 us (59%)
  Pallas kernels  48.1 us (17%)
  blocking collectives  31.3 us (11%)
  between operations  13.2 us (5%)
  local copies, waits for them, and re-layouts  13 us (5%)
  other arithmetic  8.04 us (3%)
    reduce_scatter x1, waiting for transfers between devices, body(): piece = lax.psum_scatter(partial, 'obs', scatter_dimension=0, tiled=True)  77.9 us
    all_gather x1, waiting for transfers between devices, body(): lax.all_gather(alpha_set.reshape(-1, slabs, lanes), 'bel', axis=0, tiled=...  47.7 us
    reduce_scatter x1, waiting for transfers between devices, body(): future = lax.psum_scatter(moved, 'obs', scatter_dimension=0, tiled=True)  43.7 us
    all_gather x1, blocking collectives, body(): lax.all_gather(piece[beliefs + actions:], 'obs', axis=1, tiled=True)  31.3 us
    pallas_call x1, Pallas kernels, move(): pl.pallas_call(move_kernel, grid=(actions,), out_shape=jax.ShapeDtypeStru...  24.6 us
    pallas_call x1, Pallas kernels, gather_rows(): pl.pallas_call(gather_kernel, out_shape=jax.ShapeDtypeStruct((slabs * row...  23.5 us
    unnamed x12, local copies, waits for them, and re-layouts  11.7 us
    reduce_sum x1, other arithmetic, body(): jnp.sum(transitions.astype(jnp.float32), axis=1)  7.95 us
  transfers between devices with their start and end apart: 3, of which 3 were waited for; matrix products, arithmetic and copies ran while one was open for 5% of the time, Pallas kernels for 0%

commit v1 on v0

--- a/solution.py
+++ b/solution.py
@@ -112,6 +112,622 @@
     return (actions[:, None] == jnp.arange(count, dtype=jnp.int32)[None, :]).astype(jnp.float32)
 
 
+MESH = pl.DeviceIdType.MESH
+code_top = 32767.0
+
+
+def encode(values, top):
+    q = (values * (code_top / top) + (code_top + 1.5)).astype(jnp.int32) - 32768
+    return q.astype(jnp.int16)
+
+
+def column_top(blocks):
+    tops = [jnp.max(jnp.abs(v), axis=0, keepdims=True) for v in blocks]
+    return jnp.maximum(functools.reduce(jnp.maximum, tops), 1e-30)
+
+
+def decode(codes, scale):
+    return codes.astype(jnp.int32).astype(jnp.float32) * scale
+
+
+def fused_kernel(
+    plan,
+    picks_ref,
+    act_ref,
+    actv_ref,
+    rew_ref,
+    alpha_ref,
+    w_ref,
+    trans_ref,
+    out_ref,
+    araw,
+    aslab,
+    wraw,
+    wslab,
+    tvm,
+    pick_in,
+    pick_sm,
+    stage,
+    totst,
+    totrv,
+    psend,
+    precv,
+    pscale_s,
+    pscale_r,
+    xbig,
+    outp,
+    ysum,
+    xsend,
+    xrecv,
+    xscale_s,
+    xscale_r,
+    zsend,
+    zrecv,
+    zscale_s,
+    zscale_r,
+    tpart,
+    tz,
+    tx,
+    rsel,
+    tsel,
+    loc_sem,
+    tr_sem,
+    a_ys,
+    a_yr,
+    a_ps,
+    a_pr,
+    a_fs,
+    a_fr,
+    w_xs,
+    w_xr,
+    w_fs,
+    w_fr,
+    pk_s,
+    pk_r,
+    pk_l,
+    tt_zs,
+    tt_zr,
+    tt_xs,
+    tt_xr,
+    tot_s,
+    tot_r,
+    p_s,
+    p_r,
+    ps_s,
+    ps_r,
+    x_s,
+    x_r,
+    xs_s,
+    xs_r,
+    z_s,
+    z_r,
+    zs_s,
+    zs_r,
+):
+    ranks, groups, actions, obs_local, rows, cols, beliefs, chunk, width = plan
+    zs, ys = ranks // 2, groups // 2
+    sps = cols // lanes
+    slabs = zs * sps
+    owned = beliefs // ranks
+    half_obs = obs_local // 2
+    per_row = lanes // obs_local
+    chunks = beliefs // chunk
+    steps = zs * 2 * cols // width
+
+    me_o, me_b = lax.axis_index("obs"), lax.axis_index("bel")
+    z, x = lax.div(me_o, 2), lax.rem(me_o, 2)
+    y, c = lax.div(me_b, 2), lax.rem(me_b, 2)
+    x_peer = {"obs": me_o + 1 - 2 * x}
+    core_peer = {"bel": me_b + 1 - 2 * c}
+    z_at = [lax.rem(z + d, zs) for d in range(zs)]
+    z_peer = [{"obs": zt * 2 + x} for zt in z_at]
+    y_peer = [{"bel": lax.rem(y + d, ys) * 2 + c} for d in range(ys)]
+    y_from = [lax.rem(y + ys - d, ys) for d in range(ys)]
+
+    def remote(src, dst, s_sem, r_sem, where):
+        return pltpu.make_async_remote_copy(
+            src_ref=src,
+            dst_ref=dst,
+            send_sem=s_sem,
+            recv_sem=r_sem,
+            device_id=where,
+            device_id_type=MESH,
+        )
+
+    def band(s):
+        return pl.ds(s * cols, cols)
+
+    def source_band(s, side):
+        return pl.ds(pl.multiple_of((2 * s + side) * cols, cols), cols)
+
+    own_w = [
+        pltpu.make_async_copy(
+            w_ref.at[:, :, source_band(s, x)], wraw.at[0, :, :, band(s)], loc_sem.at[0, s]
+        )
+        for s in range(zs)
+    ]
+    own_a = [
+        pltpu.make_async_copy(
+            alpha_ref.at[:, source_band(s, x)], araw.at[me_b, :, band(s)], loc_sem.at[1, s]
+        )
+        for s in range(zs)
+    ]
+    table = [
+        pltpu.make_async_copy(
+            trans_ref.at[:, pl.ds(n * width, width)], tvm.at[n], tr_sem.at[n]
+        )
+        for n in range(steps)
+    ]
+    own_pick = pltpu.make_async_copy(picks_ref, pick_sm.at[0], pk_l.at[0])
+    for copy in own_w:
+        copy.start()
+    own_pick.start()
+    for copy in own_a:
+        copy.start()
+    for copy in table:
+        copy.start()
+
+    peers = [x_peer, core_peer] + z_peer[1:] + y_peer[1:]
+    barrier = pltpu.get_barrier_semaphore()
+    for peer in peers:
+        pl.semaphore_signal(barrier, inc=1, device_id=peer, device_id_type=MESH)
+    pl.semaphore_wait(barrier, len(peers))
+
+    def half(side):
+        return pl.ds(side * half_obs, half_obs)
+
+    pick_copy = remote(picks_ref, pick_in, pk_s, pk_r, x_peer)
+    pick_copy.start()
+    w_out, a_out, a_core = [], [], []
+    for s in range(zs):
+        w_out.append(
+            remote(
+                w_ref.at[half(c), :, source_band(s, 1 - x)],
+                wraw.at[1, half(c), :, band(s)],
+                w_xs.at[s],
+                w_xr.at[s],
+                x_peer,
+            )
+        )
+        w_out[-1].start()
+        for d in range(1, ys):
+            a_out.append(
+                remote(
+                    alpha_ref.at[:, source_band(s, x)],
+                    araw.at[me_b, :, band(s)],
+                    a_ys.at[d - 1, s],
+                    a_yr.at[d - 1, s],
+                    y_peer[d],
+                )
+            )
+            a_out[-1].start()
+    for s in range(zs):
+        a_core.append(
+            remote(
+                alpha_ref.at[:, source_band(s, x)],
+                araw.at[me_b, :, band(s)],
+                a_ps.at[s],
+                a_pr.at[s],
+                core_peer,
+            )
+        )
+        a_core[-1].start()
+
+    for n in range(steps):
+        table[n].wait()
+
+        def column_total(a, carry, n=n):
+            part = tvm[n, pl.ds(pl.multiple_of(a * cols, cols), cols), :].astype(jnp.float32)
+            tpart[pl.ds(a, 1), n * width : (n + 1) * width] = jnp.sum(
+                part, axis=0, keepdims=True
+            )
+            return carry
+
+        lax.fori_loop(0, actions, column_total, 0)
+    tt_out = [
+        remote(tpart, tz.at[d - 1], tt_zs.at[d - 1], tt_zr.at[d - 1], z_peer[d])
+        for d in range(1, zs)
+    ]
+    for copy in tt_out:
+        copy.start()
+
+    def weight_slab(p, obs_from, s):
+        def one(o, carry):
+            o = o + obs_from
+            for a in range(0, actions, 8):
+                for h in range(sps):
+                    at = s * cols + h * lanes
+                    value = wraw[p, o, a : a + 8, at : at + lanes]
+                    first = ((p * obs_local + o) * actions + a) * slabs + s * sps + h
+                    wslab[pl.ds(first, 8, stride=slabs), :] = value
+            return carry
+
+        lax.fori_loop(0, half_obs, one, 0)
+
+    def alpha_slab(member, s):
+        def one(r, carry):
+            for k in range(2):
+                r0 = pl.multiple_of(r * 32 + k * 16, 16)
+                for h in range(sps):
+                    at = s * cols + h * lanes
+                    value = araw[member, pl.ds(r0, 16), at : at + lanes].astype(jnp.float32)
+                    first = (member * rows + r0) * slabs + s * sps + h
+                    aslab[pl.ds(first, 16, stride=slabs), :] = value
+            return carry
+
+        lax.fori_loop(0, rows // 32, one, 0)
+
+    for s in range(zs):
+        own_w[s].wait()
+        weight_slab(0, 0, s)
+        weight_slab(0, half_obs, s)
+    for s in range(zs):
+        own_a[s].wait()
+        alpha_slab(me_b, s)
+
+    for copy in tt_out:
+        copy.wait()
+    total = tpart[...]
+    for d in range(1, zs):
+        total = total + tz[d - 1]
+    tx[0] = total
+    tx_out = remote(tx.at[0], tx.at[1], tt_xs, tt_xr, x_peer)
+    tx_out.start()
+
+    other = me_b + 1 - 2 * c
+    for s in range(zs):
+        a_core[s].wait_recv()
+        alpha_slab(other, s)
+
+    forwards = []
+    for s in range(zs):
+        w_out[s].wait_recv()
+        forwards.append(
+            remote(
+                wraw.at[1, half(c), :, band(s)],
+                wraw.at[1, half(c), :, band(s)],
+                w_fs.at[s],
+                w_fr.at[s],
+                core_peer,
+            )
+        )
+        forwards[-1].start()
+        a_forward = []
+        for d in range(1, ys):
+            member = y_from[d] * 2 + c
+            slot = araw.at[member, :, band(s)]
+            remote(slot, slot, a_ys.at[d - 1, s], a_yr.at[d - 1, s], y_peer[d]).wait_recv()
+            a_forward.append(remote(slot, slot, a_fs.at[d - 1, s], a_fr.at[d - 1, s], core_peer))
+            a_forward[-1].start()
+        weight_slab(1, c * half_obs, s)
+        for d in range(1, ys):
+            alpha_slab(y_from[d] * 2 + c, s)
+        forwards[-1].wait_recv()
+        weight_slab(1, (1 - c) * half_obs, s)
+        for d in range(1, ys):
+            a_forward[d - 1].wait_recv()
+            alpha_slab(y_from[d] * 2 + 1 - c, s)
+        forwards += a_forward
+
+    own_pick.wait()
+    pick_copy.wait()
+    peer_pick = pltpu.make_async_copy(pick_in, pick_sm.at[1], pk_l.at[1])
+    peer_pick.start()
+    tx_out.wait()
+
+    def obs_total(a, carry):
+        sums = [None] * 4
+        for o in range(2 * obs_local):
+            term = wslab[pl.ds(pl.multiple_of((o * actions + a) * slabs, slabs), slabs), :]
+            sums[o % 4] = term if sums[o % 4] is None else sums[o % 4] + term
+        totst[pl.ds(a, slabs, stride=actions), :] = (sums[0] + sums[1]) + (sums[2] + sums[3])
+        return carry
+
+    lax.fori_loop(0, actions, obs_total, 0)
+    tot_rows = sps * actions
+    tot_out = [
+        remote(
+            totst.at[pl.ds(pl.multiple_of(z_at[d] * tot_rows, 8), tot_rows)],
+            totrv.at[d - 1],
+            tot_s.at[d - 1],
+            tot_r.at[d - 1],
+            z_peer[d],
+        )
+        for d in range(1, zs)
+    ]
+    for copy in tot_out:
+        copy.start()
+    peer_pick.wait()
+
+    p_out = []
+    for q in range(chunks):
+
+        def one(r, carry):
+            for t in range(per_row):
+                b = r * per_row + t
+                base = act_ref[b] * slabs
+                sums = [None] * 4
+                for p in range(2):
+                    for o in range(obs_local):
+                        row = aslab[
+                            pl.ds(pick_sm[p, r, t * obs_local + o], slabs), :
+                        ]
+                        at = (p * obs_local + o) * actions * slabs
+                        weight = wslab[pl.ds(base + at, slabs), :]
+                        term = row * weight
+                        k = o % 4
+                        sums[k] = term if sums[k] is None else sums[k] + term
+                stage[pl.ds(b, slabs, stride=beliefs), :] = (sums[0] + sums[1]) + (
+                    sums[2] + sums[3]
+                )
+            return carry
+
+        per_chunk = chunk // per_row
+        lax.fori_loop(q * per_chunk, (q + 1) * per_chunk, one, 0)
+        for d in range(1, zs):
+            for h in range(sps):
+                first = (z_at[d] * sps + h) * beliefs + q * chunk
+                value = stage[pl.ds(pl.multiple_of(first, 8), chunk), :]
+                top = column_top([value])
+                psend[q, d - 1, h] = encode(value, top)
+                pscale_s[q, d - 1, h : h + 1, :] = top * (1.0 / code_top)
+            here = (q, d - 1)
+            p_out.append(remote(psend.at[here], precv.at[here], p_s.at[here], p_r.at[here], z_peer[d]))
+            p_out.append(
+                remote(
+                    pscale_s.at[here], pscale_r.at[here], ps_s.at[here], ps_r.at[here], z_peer[d]
+                )
+            )
+            p_out[-1].start()
+            p_out[-2].start()
+
+    own_act = actv_ref[pl.ds(pl.multiple_of(me_o * owned, 8), owned), :]
+    block = min(512, rsel.shape[1])
+    for at in range(0, rsel.shape[1], block):
+        reward = jnp.zeros((owned, block), jnp.float32)
+        scale = jnp.zeros((owned, block), jnp.float32)
+        for a in range(actions):
+            hit = own_act == a
+            both = tx[0, a : a + 1, at : at + block] + tx[1, a : a + 1, at : at + block]
+            reward = jnp.where(hit, rew_ref[a : a + 1, at : at + block], reward)
+            scale = jnp.where(hit, both, scale)
+        rsel[:, at : at + block] = reward
+        tsel[:, at : at + block] = discount / scale
+
+    for copy in tot_out:
+        copy.wait()
+    totals = totst[pl.ds(pl.multiple_of(z * tot_rows, 8), tot_rows), :]
+    for d in range(1, zs):
+        totals = totals + totrv[d - 1]
+
+    for q in range(chunks):
+        for copy in p_out[2 * (zs - 1) * q : 2 * (zs - 1) * (q + 1)]:
+            copy.wait()
+        b0 = q * chunk
+        act = jnp.broadcast_to(actv_ref[b0 : b0 + chunk, :], (chunk, lanes))
+        for h in range(sps):
+            first = (z * sps + h) * beliefs + b0
+            value = stage[pl.ds(pl.multiple_of(first, 8), chunk), :]
+            for d in range(1, zs):
+                value = value + decode(precv[q, d - 1, h], pscale_r[q, d - 1, h : h + 1, :])
+            under = jnp.ones_like(value)
+            for a in range(actions):
+                at = h * actions + a
+                under = jnp.where(act == a, totals[at : at + 1, :], under)
+            value = value / under
+            high = value.astype(jnp.bfloat16).astype(jnp.float32)
+            low = value - high
+            for a in range(actions):
+                at = a * cols + h * lanes
+                hit = act == a
+                xbig[b0 : b0 + chunk, at : at + lanes] = jnp.where(hit, high, 0.0).astype(
+                    jnp.bfloat16
+                )
+                xbig[beliefs + b0 : beliefs + b0 + chunk, at : at + lanes] = jnp.where(
+                    hit, low, 0.0
+                ).astype(jnp.bfloat16)
+
+    def x_copies(n):
+        return (
+            remote(xsend.at[n], xrecv.at[n], x_s.at[n], x_r.at[n], x_peer),
+            remote(xscale_s.at[n], xscale_r.at[n], xs_s.at[n], xs_r.at[n], x_peer),
+        )
+
+    def z_copies(n, d):
+        here = (n, d - 1)
+        return (
+            remote(zsend.at[here], zrecv.at[here], z_s.at[here], z_r.at[here], z_peer[d]),
+            remote(zscale_s.at[here], zscale_r.at[here], zs_s.at[here], zs_r.at[here], z_peer[d]),
+        )
+
+    def owner_rows(zt, side):
+        return pl.ds(pl.multiple_of((2 * zt + side) * owned, 8), owned)
+
+    def to_pair(n):
+        sides = [outp[n, owner_rows(s, 1 - x), :] for s in range(zs)]
+        top = column_top(sides)
+        for s in range(zs):
+            xsend[n, s * owned : (s + 1) * owned, :] = encode(sides[s], top)
+        xscale_s[n] = top * (1.0 / code_top)
+        for copy in x_copies(n):
+            copy.start()
+
+    def to_owners(n):
+        for copy in x_copies(n):
+            copy.wait()
+        scale = xscale_r[n]
+        for s in range(zs):
+            part = slice(s * owned, (s + 1) * owned)
+            ysum[n, part, :] = outp[n, owner_rows(s, x), :] + decode(xrecv[n, part, :], scale)
+        for d in range(1, zs):
+            value = ysum[n, pl.ds(pl.multiple_of(z_at[d] * owned, 8), owned), :]
+            top = column_top([value])
+            zsend[n, d - 1] = encode(value, top)
+            zscale_s[n, d - 1] = top * (1.0 / code_top)
+            for copy in z_copies(n, d):
+                copy.start()
+
+    def finish(n):
+        value = ysum[n, pl.ds(pl.multiple_of(z * owned, 8), owned), :]
+        for d in range(1, zs):
+            for copy in z_copies(n, d):
+                copy.wait()
+            value = value + decode(zrecv[n, d - 1], zscale_r[n, d - 1])
+        at = pl.ds(pl.multiple_of(n * width, width), width)
+        out_ref[:, at] = rsel[:, at] + value * tsel[:, at]
+
+    lag = min(3, steps)
+
+    def step(n, carry):
+        both = jnp.dot(xbig[...], tvm[n], preferred_element_type=jnp.float32)
+        outp[n] = both[:beliefs] + both[beliefs:]
+        to_pair(n)
+
+        @pl.when(n >= 1)
+        def _():
+            to_owners(n - 1)
+
+        @pl.when(n >= lag)
+        def _():
+            finish(n - lag)
+
+        return carry
+
+    lax.fori_loop(0, steps, step, 0)
+    to_owners(steps - 1)
+    for n in range(steps - lag, steps):
+        finish(n)
+    for copy in w_out + a_out + a_core + forwards:
+        copy.wait_send()
+
+
+def fused(alpha_set, transitions, obs_weights, rewards, picks, chosen_action, groups):
+    actions, states = rewards.shape
+    obs_local = obs_weights.shape[0]
+    beliefs = chosen_action.shape[0]
+    ranks = lax.axis_size("obs")
+    rows = alpha_set.shape[0]
+    cols = states // ranks
+    zs, ys = ranks // 2, groups // 2
+    sps = cols // lanes
+    slabs = zs * sps
+    owned = beliefs // ranks
+    chunk = beliefs // 4
+    chunks = beliefs // chunk
+    width = 256
+    steps = states // width
+    xc = zs * cols
+    plan = (ranks, groups, actions, obs_local, rows, cols, beliefs, chunk, width)
+    f32, bf16, i16, i32 = jnp.float32, jnp.bfloat16, jnp.int16, jnp.int32
+    vmem, dma = pltpu.VMEM, pltpu.SemaphoreType.DMA
+    pick_rows = beliefs * obs_local // lanes
+    scratch = [
+        vmem((groups, rows, xc), bf16),
+        vmem((groups * rows * slabs, lanes), f32),
+        vmem((2, obs_local, actions, xc), f32),
+        vmem((2 * obs_local * actions * slabs, lanes), f32),
+        vmem((steps, actions * cols, width), bf16),
+        vmem((pick_rows, lanes), i32),
+        pltpu.SMEM((2, pick_rows, lanes), i32),
+        vmem((slabs * beliefs, lanes), f32),
+        vmem((slabs * actions, lanes), f32),
+        vmem((zs - 1, sps * actions, lanes), f32),
+        vmem((chunks, zs - 1, sps, chunk, lanes), i16),
+        vmem((chunks, zs - 1, sps, chunk, lanes), i16),
+        vmem((chunks, zs - 1, sps, lanes), f32),
+        vmem((chunks, zs - 1, sps, lanes), f32),
+        vmem((2 * beliefs, actions * cols), bf16),
+        vmem((steps, beliefs, width), f32),
+        vmem((steps, zs * owned, width), f32),
+        vmem((steps, zs * owned, width), i16),
+        vmem((steps, zs * owned, width), i16),
+        vmem((steps, 1, width), f32),
+        vmem((steps, 1, width), f32),
+        vmem((steps, zs - 1, owned, width), i16),
+        vmem((steps, zs - 1, owned, width), i16),
+        vmem((steps, zs - 1, 1, width), f32),
+        vmem((steps, zs - 1, 1, width), f32),
+        vmem((actions, states), f32),
+        vmem((zs - 1, actions, states), f32),
+        vmem((2, actions, states), f32),
+        vmem((owned, states), f32),
+        vmem((owned, states), f32),
+        dma((2, zs)),
+        dma((steps,)),
+        dma((max(ys - 1, 1), zs)),
+        dma((max(ys - 1, 1), zs)),
+        dma((zs,)),
+        dma((zs,)),
+        dma((max(ys - 1, 1), zs)),
+        dma((max(ys - 1, 1), zs)),
+        dma((zs,)),
+        dma((zs,)),
+        dma((zs,)),
+        dma((zs,)),
+        dma(()),
+        dma(()),
+        dma((2,)),
+        dma((zs - 1,)),
+        dma((zs - 1,)),
+        dma(()),
+        dma(()),
+        dma((zs - 1,)),
+        dma((zs - 1,)),
+        dma((chunks, zs - 1)),
+        dma((chunks, zs - 1)),
+        dma((chunks, zs - 1)),
+        dma((chunks, zs - 1)),
+        dma((steps,)),
+        dma((steps,)),
+        dma((steps,)),
+        dma((steps,)),
+        dma((steps, zs - 1)),
+        dma((steps, zs - 1)),
+        dma((steps, zs - 1)),
+        dma((steps, zs - 1)),
+    ]
+    hbm = pl.BlockSpec(memory_space=pl.ANY)
+    local = pl.BlockSpec(memory_space=pltpu.VMEM)
+    return pl.pallas_call(
+        functools.partial(fused_kernel, plan),
+        out_shape=jax.ShapeDtypeStruct((owned, states), f32),
+        in_specs=[hbm, pl.BlockSpec(memory_space=pltpu.SMEM), local, local, hbm, hbm, hbm],
+        out_specs=local,
+        scratch_shapes=scratch,
+        compiler_params=pltpu.CompilerParams(
+            collective_id=0, has_side_effects=True, vmem_limit_bytes=67043328
+        ),
+        name="backup",
+    )(
+        (picks * slabs).reshape(pick_rows, lanes),
+        chosen_action,
+        chosen_action[:, None],
+        rewards,
+        alpha_set,
+        obs_weights,
+        transitions.reshape(actions * cols, states),
+    )
+
+
+def fits(alpha_set, transitions, obs_weights, beliefs, ranks, groups):
+    cols = transitions.shape[1]
+    obs_local, actions, states = obs_weights.shape
+    return (
+        ranks % 2 == 0
+        and ranks > 2
+        and groups % 2 == 0
+        and cols % lanes == 0
+        and states == ranks * cols
+        and states % 256 == 0
+        and actions % 8 == 0
+        and obs_local % 2 == 0
+        and lanes % obs_local == 0
+        and alpha_set.shape[0] % 32 == 0
+        and beliefs % (16 * ranks) == 0
+        and beliefs % 64 == 0
+    )
+
+
 def body(alpha_set, transitions, obs_weights, rewards, chosen_idx, chosen_action):
     actions, states = rewards.shape
     obs_local = obs_weights.shape[0]
@@ -120,6 +736,11 @@
     ranks = lax.axis_size("obs")
     action_hot = action_table(chosen_action, actions)
     picks = jnp.sum(jnp.where(action_hot[:, :, None] > 0, chosen_idx, 0), axis=1).reshape(-1)
+    groups = lax.axis_size("bel")
+    if fits(alpha_set, transitions, obs_weights, beliefs, ranks, groups):
+        return fused(
+            alpha_set, transitions, obs_weights, rewards, picks, chosen_action, groups
+        )
     alpha = lax.all_gather(alpha_set.reshape(-1, slabs, lanes), "bel", axis=0, tiled=True)
     weights = obs_weights.reshape(obs_local * actions, slabs, lanes)
     trans_part = jnp.sum(transitions.astype(jnp.float32), axis=1).reshape(actions, slabs, lanes)

time: 286 us -> 111 us (0.39)
  waiting for transfers between devices: 169 us -> 0 us
  Pallas kernels: 48.1 us -> 105 us
  blocking collectives: 31.3 us -> 0 us
  between operations: 13.2 us -> 0.03 us
  local copies, waits for them, and re-layouts: 13 us -> 4.09 us
  other arithmetic: 8.04 us -> 1.91 us
    reduce_scatter x2 -> x0, waiting for transfers between devices: 122 us -> none  [the longest x1 77.9 us: body(): piece = lax.psum_scatter(partial, 'obs', scatter_dimension=0, tiled=True)]
    pallas_call x2 -> x1, Pallas kernels: 48.1 us -> 105 us  [fused(): pl.pallas_call(functools.partial(fused_kernel, plan), out_shape=jax.Shape...]
    all_gather x1 -> x0, waiting for transfers between devices: 47.7 us -> none  [body(): lax.all_gather(alpha_set.reshape(-1, slabs, lanes), 'bel', axis=0, tiled=...]
    all_gather x1 -> x0, blocking collectives: 31.3 us -> none  [body(): lax.all_gather(piece[beliefs + actions:], 'obs', axis=1, tiled=True)]
    unnamed x12 -> x1, local copies, waits for them, and re-layouts: 11.7 us -> 1.77 us
    reduce_sum x1 -> x0, other arithmetic: 7.95 us -> none  [body(): jnp.sum(transitions.astype(jnp.float32), axis=1)]
  transfers between devices with their start and end apart: 3 -> 0, of which waited for: 3 -> 0; matrix products, arithmetic and copies ran while one was open for 5% -> 0% of each run, Pallas kernels for 0% -> 0%
where the time goes in v1:
time: 111 us
  Pallas kernels  105 us (95%)
  local copies, waits for them, and re-layouts  4.09 us (4%)
  other arithmetic  1.91 us (2%)
    pallas_call x1, Pallas kernels, fused(): pl.pallas_call(functools.partial(fused_kernel, plan), out_shape=jax.Shape...  105 us

profile of v1, /device:TPU:0, one launch (start us, length us, event | category | flops | bytes accessed | tf_op | source)
XLA Modules:
  0.0 111.1 jit_solution(14239135906719063320)
XLA Ops:
  0.0 0.7 convert_compare_fusion
  0.7 1.2 %select_reduce_fusion = s32[384,32]{0,1:T(8,128)S(1)} fusion(s32[384,16,32]{0,2,1:T(8,128)} %param.10, pred[384,16]{0,1:T(8,128)(4,1)S(1)} %convert_compare_fusion), kind=kLoop, calls=%fused_computation | loop fusion | flops 380928 | bytes 841728 | tf_op jit(solution)/shard_map/reduce_sum | solution.py:738
  1.9 0.1 copy.8
  2.0 0.7 mul.12.picks_ref
  2.8 1.5 %broadcast_in_dim.21.actv_ref = s32[384,1]{1,0:T(8,128)} reshape(s32[384]{0:T(512)} %act_ref.1) | data formatting | bytes 3072 | tf_op jit(solution)/shard_map/broadcast_in_dim | solution.py:112
  4.3 105.1 %backup.1 = f32[48,2048]{1,0:T(8,128)} custom-call(s32[96,128]{1,0:T(8,128)} %mul.12.picks_ref, s32[384]{0:T(512)} %act_ref.1, s32[384,1]{1,0:T(8,128)} %broadcast_in_dim.21.actv_ref, f32[16,2048]{1,0:T(8,128)} %rew_ref.1, bf16[512,2048]{1,0:T(8,128)(2,1)} %alpha_ref.1, f32[32,16,2048]{2,1,0:T(8,128)} %w_ref.1, bf16[4096,2048]{1,0:T(8,128)(2,1)} %bitcast.1), custom_call_target="tpu_custom_call" | custom-call | tf_op jit(solution)/shard_map/backup/pallas_call | solution.py:691
  109.4 1.8 %copy.11 = f32[48,2048]{1,0:T(8,128)} copy(f32[48,2048]{1,0:T(8,128)} %backup.1) | data formatting | bytes 786432
  (1 shorter events, 0.0 us)

commit v2 on v0

--- a/solution.py
+++ b/solution.py
@@ -1,4 +1,5 @@
 import functools
+import types
 
 import jax
 import jax.numpy as jnp
@@ -112,12 +113,712 @@
     return (actions[:, None] == jnp.arange(count, dtype=jnp.int32)[None, :]).astype(jnp.float32)
 
 
+MESH = pl.DeviceIdType.MESH
+code_top = 32767.0
+
+
+def encode(values, top):
+    q = (values * (code_top / top) + (code_top + 1.5)).astype(jnp.int32) - 32768
+    return q.astype(jnp.int16)
+
+
+def column_top(blocks):
+    tops = [jnp.max(jnp.abs(v), axis=0, keepdims=True) for v in blocks]
+    return jnp.maximum(functools.reduce(jnp.maximum, tops), 1e-30)
+
+
+def decode(codes, scale):
+    return codes.astype(jnp.int32).astype(jnp.float32) * scale
+
+
+def fused_kernel(plan, names, *refs):
+    r = types.SimpleNamespace(**dict(zip(names, refs)))
+    ranks, groups, actions, obs_local, rows, cols, beliefs, chunk, width = plan
+    zs, ys = ranks // 2, groups // 2
+    sps = cols // lanes
+    slabs = zs * sps
+    owned = beliefs // ranks
+    half_obs = obs_local // 2
+    chunks = beliefs // chunk
+    steps = zs * 2 * cols // width
+    share = steps // groups
+    parts = r.a_yr.shape[2]
+    part_rows = rows // parts
+    pairs = zs // 2
+
+    me_o, me_b = lax.axis_index("obs"), lax.axis_index("bel")
+    z, x = lax.div(me_o, 2), lax.rem(me_o, 2)
+    y, c = lax.div(me_b, 2), lax.rem(me_b, 2)
+    odd = lax.rem(z, 2)
+    other = me_b + 1 - 2 * c
+    x_peer = {"obs": me_o + 1 - 2 * x}
+    core_peer = {"bel": other}
+    next_z = {"obs": (z + 1 - 2 * odd) * 2 + x}
+    z_at = [lax.rem(z + d, zs) for d in range(zs)]
+    z_peer = [{"obs": zt * 2 + x} for zt in z_at]
+    y_peer = [{"bel": lax.rem(y + d, ys) * 2 + c} for d in range(ys)]
+    y_from = [lax.rem(y + ys - d, ys) for d in range(ys)]
+    b_peer = [{"bel": lax.rem(me_b + d, groups)} for d in range(groups)]
+    b_from = [lax.rem(me_b + groups - d, groups) for d in range(groups)]
+
+    def remote(src, dst, s_sem, r_sem, where):
+        return pltpu.make_async_remote_copy(
+            src_ref=src,
+            dst_ref=dst,
+            send_sem=s_sem,
+            recv_sem=r_sem,
+            device_id=where,
+            device_id_type=MESH,
+        )
+
+    def band(s):
+        return pl.ds(pl.multiple_of(s * cols, lanes), cols)
+
+    def source_band(s, side):
+        return pl.ds(pl.multiple_of((2 * s + side) * cols, lanes), cols)
+
+    def half(side):
+        return pl.ds(side * half_obs, half_obs)
+
+    own_idx = pltpu.make_async_copy(r.idx, r.idx_in, r.pk_l.at[2 * obs_local])
+    peer_w = [
+        pltpu.make_async_copy(
+            r.weights.at[half(c), :, source_band(s, 1 - x)], r.w_src.at[s], r.loc_sem.at[2, s]
+        )
+        for s in range(zs)
+    ]
+    own_w = [
+        pltpu.make_async_copy(
+            r.weights.at[:, :, source_band(s, x)], r.wraw.at[:, :, band(s)], r.loc_sem.at[0, s]
+        )
+        for s in range(zs)
+    ]
+    own_a = [
+        pltpu.make_async_copy(
+            r.alpha.at[:, source_band(s, x)], r.araw.at[me_b, :, band(s)], r.loc_sem.at[1, s]
+        )
+        for s in range(zs)
+    ]
+    table = []
+    for k in range(steps):
+        n = lax.rem(me_b * share + k, steps)
+        at = pl.ds(pl.multiple_of(n * width, lanes), width)
+        table.append(pltpu.make_async_copy(r.trans.at[:, at], r.tvm.at[n], r.tr_sem.at[k]))
+    for copy in peer_w + [own_idx] + own_w + table[:share] + own_a + table[share:]:
+        copy.start()
+
+    peers = [x_peer] + z_peer[1:] + b_peer[1:]
+    barrier = pltpu.get_barrier_semaphore()
+    for peer in peers:
+        pl.semaphore_signal(barrier, inc=1, device_id=peer, device_id_type=MESH)
+    pl.semaphore_wait(barrier, len(peers))
+
+    def rows_of(h):
+        return pl.ds(h * part_rows, part_rows)
+
+    def near(k):
+        return 2 * k + odd
+
+    def far(k):
+        return 2 * k + 1 - odd
+
+    pieces = [(k, h) for k in range(pairs) for h in range(parts)]
+    sent = []
+
+    def launch(copy):
+        copy.start()
+        sent.append(copy)
+
+    for k, h in pieces:
+        for d in range(1, ys):
+            launch(
+                remote(
+                    r.alpha.at[rows_of(h), source_band(near(k), x)],
+                    r.araw.at[me_b, rows_of(h), band(near(k))],
+                    r.a_ys.at[d - 1, k, h],
+                    r.a_yr.at[d - 1, k, h],
+                    y_peer[d],
+                )
+            )
+    a_core = [
+        remote(
+            r.alpha.at[:, source_band(s, x)],
+            r.araw.at[me_b, :, band(s)],
+            r.a_ps.at[s],
+            r.a_pr.at[s],
+            core_peer,
+        )
+        for s in range(zs)
+    ]
+    for copy in a_core:
+        launch(copy)
+
+    w_out = []
+    for s in range(zs):
+        peer_w[s].wait()
+        for at in range(0, cols, lanes):
+            value = r.w_src[s, :, :, at : at + lanes]
+            top = jnp.maximum(jnp.max(jnp.abs(value), axis=0), 1e-30)
+            r.w_code_s[s, :, :, at : at + lanes] = encode(value, top[None])
+            r.w_scale_s[s, :, at : at + lanes] = top * (1.0 / code_top)
+        w_out.append(
+            (
+                remote(r.w_code_s.at[s], r.w_code.at[c, s], r.w_xs.at[0, s], r.w_xr.at[0, s], x_peer),
+                remote(
+                    r.w_scale_s.at[s], r.w_scale.at[c, s], r.w_xs.at[1, s], r.w_xr.at[1, s], x_peer
+                ),
+            )
+        )
+        for copy in w_out[-1]:
+            launch(copy)
+
+    pick_sm = [getattr(r, f"pick_{k}") for k in range(2 * obs_local)]
+    waiting = []
+
+    def store_picks(source, first):
+        for o in range(obs_local):
+            copy = pltpu.make_async_copy(
+                source.at[pl.ds(o, 1), :], pick_sm[first + o], r.pk_l.at[first + o]
+            )
+            copy.start()
+            waiting.append(copy)
+
+    def own_picks():
+        own_idx.wait()
+        action_row = r.act_row[...]
+        chosen = jnp.zeros((obs_local, beliefs), jnp.int32)
+        for a in range(actions):
+            chosen = jnp.where(action_row == a, r.idx_in[a], chosen)
+        r.pick_out[...] = chosen * slabs
+
+    pick_copy = remote(r.pick_out, r.pick_in, r.pk_s, r.pk_r, x_peer)
+    tt_out = [
+        remote(r.tpart, r.tz.at[d - 1], r.tt_zs.at[d - 1], r.tt_zr.at[d - 1], z_peer[d])
+        for d in range(1, zs)
+    ]
+    tx_out = remote(r.tx.at[0], r.tx.at[1], r.tt_xs, r.tt_xr, x_peer)
+
+    def transition_totals():
+        for k in range(share):
+            table[k].wait()
+            n = me_b * share + k
+
+            def column_total(a, carry, n=n, k=k):
+                value = r.tvm[n, pl.ds(pl.multiple_of(a * cols, 16), cols), :].astype(jnp.float32)
+                r.tpart[pl.ds(a, 1), k * width : (k + 1) * width] = jnp.sum(
+                    value, axis=0, keepdims=True
+                )
+                return carry
+
+            lax.fori_loop(0, actions, column_total, 0)
+
+    def action_lanes(b, carry):
+        r.actb[pl.ds(b, 1), :] = jnp.full((1, lanes), r.act[b], jnp.int32)
+        return carry
+
+    pad = slabs
+
+    def own_weight_slab(s):
+        def one(o, carry):
+            for h in range(sps):
+                at = s * cols + h * lanes
+                first = o * actions * slabs + s * sps + h + pad
+                r.wslab[pl.ds(first, actions, stride=slabs), :] = r.wraw[o, :, at : at + lanes]
+            return carry
+
+        lax.fori_loop(0, obs_local, one, 0)
+
+    def peer_weight_slab(side, s):
+        def one(o, carry):
+            for h in range(sps):
+                at = slice(h * lanes, (h + 1) * lanes)
+                first = (obs_local + side * half_obs + o) * actions * slabs + s * sps + h + pad
+                r.wslab[pl.ds(first, actions, stride=slabs), :] = decode(
+                    r.w_code[side, s, o, :, at], r.w_scale[side, s, :, at]
+                )
+            return carry
+
+        lax.fori_loop(0, half_obs, one, 0)
+
+    def alpha_slab(member, s, first_row, count):
+        def one(i, carry):
+            for k in range(2):
+                r0 = pl.multiple_of(first_row + i * 32 + k * 16, 16)
+                for h in range(sps):
+                    at = pl.ds(pl.multiple_of(s * cols + h * lanes, lanes), lanes)
+                    first = (member * rows + r0) * slabs + s * sps + h
+                    r.aslab[pl.ds(first, 16, stride=slabs), :] = r.araw[
+                        member, pl.ds(r0, 16), at
+                    ].astype(jnp.float32)
+            return carry
+
+        lax.fori_loop(0, count // 32, one, 0)
+
+    late = []
+
+    def arrived(k, h, by_z):
+        s = far(k) if by_z else near(k)
+        for d in range(1, ys):
+            member = y_from[d] * 2 + c
+            slot = r.araw.at[member, rows_of(h), band(s)]
+            here = (d - 1, k, h)
+            if by_z:
+                remote(slot, slot, r.a_zs.at[here], r.a_zr.at[here], next_z).wait_recv()
+            else:
+                remote(slot, slot, r.a_ys.at[here], r.a_yr.at[here], y_peer[d]).wait_recv()
+                launch(remote(slot, slot, r.a_zs.at[here], r.a_zr.at[here], next_z))
+            at = (d - 1, int(by_z), k, h)
+            forward = remote(slot, slot, r.a_fs.at[at], r.a_fr.at[at], core_peer)
+            launch(forward)
+            alpha_slab(member, s, h * part_rows, part_rows)
+
+            def rest(forward=forward, member=y_from[d] * 2 + 1 - c):
+                forward.wait_recv()
+                alpha_slab(member, s, h * part_rows, part_rows)
+
+            late.append(rest)
+
+    def weights_arrived(s):
+        both = []
+        for k, copy in enumerate(w_out[s]):
+            copy.wait_recv()
+            held = (r.w_code, r.w_scale)[k].at[c, s]
+            both.append(remote(held, held, r.w_fs.at[k, s], r.w_fr.at[k, s], core_peer))
+            launch(both[-1])
+        peer_weight_slab(c, s)
+
+        def rest():
+            for copy in both:
+                copy.wait_recv()
+            peer_weight_slab(1 - c, s)
+
+        late.append(rest)
+
+    count = len(pieces)
+    for i in range(count + 1):
+        ready, late = late, []
+        if i < count:
+            arrived(*pieces[i], False)
+        if i >= 1:
+            arrived(*pieces[i - 1], True)
+        for s in range(i * zs // (count + 1), (i + 1) * zs // (count + 1)):
+            weights_arrived(s)
+        for rest in ready:
+            rest()
+        if i == 0:
+            own_picks()
+            for s in range(zs):
+                own_w[s].wait()
+                own_weight_slab(s)
+            pick_copy.start()
+            store_picks(r.pick_out, 0)
+            for s in range(zs):
+                own_a[s].wait()
+                alpha_slab(me_b, s, 0, rows)
+        if i == 1:
+            transition_totals()
+            for s in range(zs):
+                a_core[s].wait_recv()
+                alpha_slab(other, s, 0, rows)
+            for copy in tt_out:
+                copy.start()
+        if i == 2:
+            pick_copy.wait()
+            store_picks(r.pick_in, obs_local)
+            lax.fori_loop(0, beliefs, action_lanes, 0, unroll=8)
+    for rest in late:
+        rest()
+    for copy in tt_out:
+        copy.wait()
+    total = r.tpart[...]
+    for d in range(1, zs):
+        total = total + r.tz[d - 1]
+    r.tx[0] = total
+
+    def obs_total(a, carry):
+        sums = [None] * 4
+        for o in range(2 * obs_local):
+            term = r.wslab[pl.ds(pl.multiple_of((o * actions + a) * slabs + pad, slabs), slabs), :]
+            sums[o % 4] = term if sums[o % 4] is None else sums[o % 4] + term
+        r.totst[pl.ds(a, slabs, stride=actions), :] = (sums[0] + sums[1]) + (sums[2] + sums[3])
+        return carry
+
+    lax.fori_loop(0, actions, obs_total, 0)
+    tot_rows = sps * actions
+    tot_out = [
+        remote(
+            r.totst.at[pl.ds(pl.multiple_of(z_at[d] * tot_rows, 8), tot_rows)],
+            r.totrv.at[d - 1],
+            r.tot_s.at[d - 1],
+            r.tot_r.at[d - 1],
+            z_peer[d],
+        )
+        for d in range(1, zs)
+    ]
+    tall_out = [
+        remote(
+            r.tall.at[me_b], r.tall.at[me_b], r.tall_s.at[d - 1], r.tall_r.at[d - 1], b_peer[d]
+        )
+        for d in range(1, groups)
+    ]
+    for copy in tot_out + [tx_out]:
+        copy.start()
+    for copy in waiting:
+        copy.wait()
+
+    def share_totals():
+        tx_out.wait()
+        r.tall[me_b] = r.tx[0] + r.tx[1]
+        for copy in tall_out:
+            copy.start()
+
+    def p_copies(q, d):
+        here = (q, d - 1)
+        return (
+            remote(r.psend.at[here], r.precv.at[here], r.p_s.at[here], r.p_r.at[here], z_peer[d]),
+            remote(
+                r.pscale_s.at[here], r.pscale_r.at[here], r.ps_s.at[here], r.ps_r.at[here], z_peer[d]
+            ),
+        )
+
+    unroll = 4
+
+    def gather_chunk(q):
+        def one(i, carry):
+            for t in range(unroll):
+                b = q * chunk + i * unroll + t
+                base = r.act[b] * slabs
+                sums = [None] * 4
+                for p in range(2):
+                    for o in range(obs_local):
+                        row = r.aslab[pl.ds(pick_sm[p * obs_local + o][0, b], slabs), :]
+                        at = (p * obs_local + o) * actions * slabs + pad
+                        term = row * r.wslab[pl.ds(base + at, slabs), :]
+                        k = o % 4
+                        sums[k] = term if sums[k] is None else sums[k] + term
+                r.stage[pl.ds(b, slabs, stride=beliefs), :] = (sums[0] + sums[1]) + (
+                    sums[2] + sums[3]
+                )
+            return carry
+
+        lax.fori_loop(0, chunk // unroll, one, 0)
+        for d in range(1, zs):
+            for h in range(sps):
+                first = (z_at[d] * sps + h) * beliefs + q * chunk
+                value = r.stage[pl.ds(pl.multiple_of(first, 8), chunk), :]
+                top = column_top([value])
+                r.psend[q, d - 1, h] = encode(value, top)
+                r.pscale_s[q, d - 1, h : h + 1, :] = top * (1.0 / code_top)
+            for copy in p_copies(q, d):
+                copy.start()
+
+    def prepare():
+        for copy in tot_out + tall_out:
+            copy.wait()
+        totals = r.totst[pl.ds(pl.multiple_of(z * tot_rows, 8), tot_rows), :]
+        for d in range(1, zs):
+            totals = totals + r.totrv[d - 1]
+        r.tsum[...] = totals
+        own_act = r.actb[pl.ds(pl.multiple_of(me_o * owned, 8), owned), :]
+        per_member = share * width // lanes
+
+        for member in range(groups):
+            for k in range(per_member):
+                at = slice(k * lanes, (k + 1) * lanes)
+                to = slice((member * per_member + k) * lanes, (member * per_member + k + 1) * lanes)
+                reward = jnp.zeros((owned, lanes), jnp.float32)
+                scale = jnp.ones((owned, lanes), jnp.float32)
+                for a in range(actions):
+                    hit = own_act == a
+                    reward = jnp.where(hit, r.rew[a : a + 1, to], reward)
+                    scale = jnp.where(hit, r.tall[member, a : a + 1, at], scale)
+                r.rsel[:, to] = reward
+                r.tsel[:, to] = discount / scale
+
+    def absorb(q):
+        for d in range(1, zs):
+            for copy in p_copies(q, d):
+                copy.wait()
+        b0 = pl.multiple_of(q * chunk, 16)
+        act = r.actb[pl.ds(b0, chunk), :]
+        for h in range(sps):
+            first = (z * sps + h) * beliefs + q * chunk
+            value = r.stage[pl.ds(pl.multiple_of(first, 8), chunk), :]
+            for d in range(1, zs):
+                value = value + decode(r.precv[q, d - 1, h], r.pscale_r[q, d - 1, h : h + 1, :])
+            under = jnp.ones_like(value)
+            for a in range(actions):
+                at = h * actions + a
+                under = jnp.where(act == a, r.tsum[at : at + 1, :], under)
+            value = value / under
+            high = value.astype(jnp.bfloat16).astype(jnp.float32)
+            low = value - high
+            for a in range(actions):
+                at = slice(a * cols + h * lanes, a * cols + (h + 1) * lanes)
+                hit = act == a
+                r.xbig[pl.ds(b0, chunk), at] = jnp.where(hit, high, 0.0).astype(jnp.bfloat16)
+                r.xbig[pl.ds(pl.multiple_of(beliefs + b0, 16), chunk), at] = jnp.where(
+                    hit, low, 0.0
+                ).astype(jnp.bfloat16)
+
+    behind = min(3, chunks - 1)
+
+    def gather_step(q, carry):
+        gather_chunk(q)
+
+        @pl.when(q == 0)
+        def _():
+            share_totals()
+
+        @pl.when(q == behind - 1)
+        def _():
+            prepare()
+
+        @pl.when(q >= behind)
+        def _():
+            absorb(q - behind)
+
+        return carry
+
+    lax.fori_loop(0, chunks, gather_step, 0)
+
+    def absorb_step(q, carry):
+        absorb(q)
+        return carry
+
+    lax.fori_loop(chunks - behind, chunks, absorb_step, 0)
+    for copy in table[share:]:
+        copy.wait()
+
+    def x_copies(n):
+        return (
+            remote(r.xsend.at[n], r.xrecv.at[n], r.x_s.at[n], r.x_r.at[n], x_peer),
+            remote(r.xscale_s.at[n], r.xscale_r.at[n], r.xs_s.at[n], r.xs_r.at[n], x_peer),
+        )
+
+    def z_copies(n, d):
+        here = (n, d - 1)
+        return (
+            remote(r.zsend.at[here], r.zrecv.at[here], r.z_s.at[here], r.z_r.at[here], z_peer[d]),
+            remote(r.zscale_s.at[here], r.zscale_r.at[here], r.zs_s.at[here], r.zs_r.at[here], z_peer[d]),
+        )
+
+    def owner_rows(zt, side):
+        return pl.ds(pl.multiple_of((2 * zt + side) * owned, 8), owned)
+
+    def to_pair(n):
+        sides = [r.outp[n, owner_rows(s, 1 - x), :] for s in range(zs)]
+        top = column_top(sides)
+        for s in range(zs):
+            r.xsend[n, s * owned : (s + 1) * owned, :] = encode(sides[s], top)
+        r.xscale_s[n] = top * (1.0 / code_top)
+        for copy in x_copies(n):
+            copy.start()
+
+    def to_owners(n):
+        for copy in x_copies(n):
+            copy.wait()
+        scale = r.xscale_r[n]
+        for s in range(zs):
+            part = slice(s * owned, (s + 1) * owned)
+            r.ysum[n, part, :] = r.outp[n, owner_rows(s, x), :] + decode(r.xrecv[n, part, :], scale)
+        for d in range(1, zs):
+            value = r.ysum[n, pl.ds(pl.multiple_of(z_at[d] * owned, 8), owned), :]
+            top = column_top([value])
+            r.zsend[n, d - 1] = encode(value, top)
+            r.zscale_s[n, d - 1] = top * (1.0 / code_top)
+            for copy in z_copies(n, d):
+                copy.start()
+
+    def finish(n):
+        value = r.ysum[n, pl.ds(pl.multiple_of(z * owned, 8), owned), :]
+        for d in range(1, zs):
+            for copy in z_copies(n, d):
+                copy.wait()
+            value = value + decode(r.zrecv[n, d - 1], r.zscale_r[n, d - 1])
+        at = pl.ds(pl.multiple_of(n * width, width), width)
+        r.out[:, at] = r.rsel[:, at] + value * r.tsel[:, at]
+
+    pair_lag, lag = min(2, steps), min(5, steps)
+
+    def step(n, carry):
+        both = jnp.dot(r.xbig[...], r.tvm[n], preferred_element_type=jnp.float32)
+        r.outp[n] = both[:beliefs] + both[beliefs:]
+        to_pair(n)
+
+        @pl.when(n >= pair_lag)
+        def _():
+            to_owners(n - pair_lag)
+
+        @pl.when(n >= lag)
+        def _():
+            finish(n - lag)
+
+        return carry
+
+    lax.fori_loop(0, steps, step, 0)
+    for n in range(steps - pair_lag, steps):
+        to_owners(n)
+    for n in range(steps - lag, steps):
+        finish(n)
+    for copy in sent:
+        copy.wait_send()
+
+
+def fused(alpha_set, transitions, obs_weights, rewards, chosen_idx, chosen_action, groups):
+    actions, states = rewards.shape
+    obs_local = obs_weights.shape[0]
+    beliefs = chosen_action.shape[0]
+    ranks = lax.axis_size("obs")
+    rows = alpha_set.shape[0]
+    cols = states // ranks
+    zs, ys = ranks // 2, groups // 2
+    sps = cols // lanes
+    slabs = zs * sps
+    owned = beliefs // ranks
+    half_obs = obs_local // 2
+    chunks = 8
+    chunk = beliefs // chunks
+    width = 256
+    steps = states // width
+    xc = zs * cols
+    shared = states // groups
+    outer, parts, pairs = max(ys - 1, 1), 2, zs // 2
+    plan = (ranks, groups, actions, obs_local, rows, cols, beliefs, chunk, width)
+    f32, bf16, i16, i32 = jnp.float32, jnp.bfloat16, jnp.int16, jnp.int32
+    vmem, dma = pltpu.VMEM, pltpu.SemaphoreType.DMA
+    scratch = dict(
+        idx_in=vmem((actions, obs_local, beliefs), i32),
+        araw=vmem((groups, rows, xc), bf16),
+        aslab=vmem((groups * rows * slabs, lanes), f32),
+        wraw=vmem((obs_local, actions, xc), f32),
+        w_src=vmem((zs, half_obs, actions, cols), f32),
+        w_code_s=vmem((zs, half_obs, actions, cols), i16),
+        w_scale_s=vmem((zs, actions, cols), f32),
+        w_code=vmem((2, zs, half_obs, actions, cols), i16),
+        w_scale=vmem((2, zs, actions, cols), f32),
+        wslab=vmem(((2 * obs_local * actions + 1) * slabs, lanes), f32),
+        tvm=vmem((steps, actions * cols, width), bf16),
+        pick_out=vmem((obs_local, beliefs), i32),
+        pick_in=vmem((obs_local, beliefs), i32),
+        actb=vmem((beliefs, lanes), i32),
+        stage=vmem((slabs * beliefs, lanes), f32),
+        totst=vmem((slabs * actions, lanes), f32),
+        totrv=vmem((zs - 1, sps * actions, lanes), f32),
+        tsum=vmem((sps * actions, lanes), f32),
+        psend=vmem((chunks, zs - 1, sps, chunk, lanes), i16),
+        precv=vmem((chunks, zs - 1, sps, chunk, lanes), i16),
+        pscale_s=vmem((chunks, zs - 1, sps, lanes), f32),
+        pscale_r=vmem((chunks, zs - 1, sps, lanes), f32),
+        xbig=vmem((2 * beliefs, actions * cols), bf16),
+        outp=vmem((steps, beliefs, width), f32),
+        ysum=vmem((steps, zs * owned, width), f32),
+        xsend=vmem((steps, zs * owned, width), i16),
+        xrecv=vmem((steps, zs * owned, width), i16),
+        xscale_s=vmem((steps, 1, width), f32),
+        xscale_r=vmem((steps, 1, width), f32),
+        zsend=vmem((steps, zs - 1, owned, width), i16),
+        zrecv=vmem((steps, zs - 1, owned, width), i16),
+        zscale_s=vmem((steps, zs - 1, 1, width), f32),
+        zscale_r=vmem((steps, zs - 1, 1, width), f32),
+        tpart=vmem((actions, shared), f32),
+        tz=vmem((zs - 1, actions, shared), f32),
+        tx=vmem((2, actions, shared), f32),
+        tall=vmem((groups, actions, shared), f32),
+        rsel=vmem((owned, states), f32),
+        tsel=vmem((owned, states), f32),
+        **{f"pick_{k}": pltpu.SMEM((1, beliefs), i32) for k in range(2 * obs_local)},
+        pk_l=dma((2 * obs_local + 1,)),
+        loc_sem=dma((3, zs)),
+        tr_sem=dma((steps,)),
+        a_ys=dma((outer, pairs, parts)),
+        a_yr=dma((outer, pairs, parts)),
+        a_zs=dma((outer, pairs, parts)),
+        a_zr=dma((outer, pairs, parts)),
+        a_fs=dma((outer, 2, pairs, parts)),
+        a_fr=dma((outer, 2, pairs, parts)),
+        a_ps=dma((zs,)),
+        a_pr=dma((zs,)),
+        w_xs=dma((2, zs)),
+        w_xr=dma((2, zs)),
+        w_fs=dma((2, zs)),
+        w_fr=dma((2, zs)),
+        pk_s=dma(()),
+        pk_r=dma(()),
+        tt_zs=dma((zs - 1,)),
+        tt_zr=dma((zs - 1,)),
+        tt_xs=dma(()),
+        tt_xr=dma(()),
+        tall_s=dma((groups - 1,)),
+        tall_r=dma((groups - 1,)),
+        tot_s=dma((zs - 1,)),
+        tot_r=dma((zs - 1,)),
+        p_s=dma((chunks, zs - 1)),
+        p_r=dma((chunks, zs - 1)),
+        ps_s=dma((chunks, zs - 1)),
+        ps_r=dma((chunks, zs - 1)),
+        x_s=dma((steps,)),
+        x_r=dma((steps,)),
+        xs_s=dma((steps,)),
+        xs_r=dma((steps,)),
+        z_s=dma((steps, zs - 1)),
+        z_r=dma((steps, zs - 1)),
+        zs_s=dma((steps, zs - 1)),
+        zs_r=dma((steps, zs - 1)),
+    )
+    hbm = pl.BlockSpec(memory_space=pl.ANY)
+    smem = pl.BlockSpec(memory_space=pltpu.SMEM)
+    local = pl.BlockSpec(memory_space=pltpu.VMEM)
+    names = ("act", "act_row", "rew", "idx", "alpha", "weights", "trans", "out", *scratch)
+    return pl.pallas_call(
+        functools.partial(fused_kernel, plan, names),
+        out_shape=jax.ShapeDtypeStruct((owned, states), f32),
+        in_specs=[smem, local, local, hbm, hbm, hbm, hbm],
+        out_specs=local,
+        scratch_shapes=list(scratch.values()),
+        compiler_params=pltpu.CompilerParams(
+            collective_id=0, has_side_effects=True, vmem_limit_bytes=67043328
+        ),
+        name="backup",
+    )(
+        chosen_action,
+        chosen_action[None, :],
+        rewards,
+        chosen_idx.transpose(1, 2, 0),
+        alpha_set,
+        obs_weights,
+        transitions.reshape(actions * cols, states),
+    )
+
+
+def fits(alpha_set, transitions, obs_weights, beliefs, ranks, groups):
+    cols = transitions.shape[1]
+    obs_local, actions, states = obs_weights.shape
+    return (
+        ranks % 4 == 0
+        and groups % 2 == 0
+        and cols % lanes == 0
+        and states == ranks * cols
+        and states % (256 * groups) == 0
+        and actions % 8 == 0
+        and obs_local % 2 == 0
+        and alpha_set.shape[0] % 64 == 0
+        and beliefs % (16 * ranks) == 0
+        and beliefs % 128 == 0
+    )
+
+
 def body(alpha_set, transitions, obs_weights, rewards, chosen_idx, chosen_action):
     actions, states = rewards.shape
     obs_local = obs_weights.shape[0]
     beliefs = chosen_action.shape[0]
     slabs = states // lanes
     ranks = lax.axis_size("obs")
+    groups = lax.axis_size("bel")
+    if fits(alpha_set, transitions, obs_weights, beliefs, ranks, groups):
+        return fused(
+            alpha_set, transitions, obs_weights, rewards, chosen_idx, chosen_action, groups
+        )
     action_hot = action_table(chosen_action, actions)
     picks = jnp.sum(jnp.where(action_hot[:, :, None] > 0, chosen_idx, 0), axis=1).reshape(-1)
     alpha = lax.all_gather(alpha_set.reshape(-1, slabs, lanes), "bel", axis=0, tiled=True)

time: 286 us -> 89.1 us (0.31)
  waiting for transfers between devices: 169 us -> 0 us
  Pallas kernels: 48.1 us -> 85.9 us
  blocking collectives: 31.3 us -> 0 us
  between operations: 13.2 us -> 0.01 us
  local copies, waits for them, and re-layouts: 13 us -> 3.01 us
  other arithmetic: 8.04 us -> 0 us
    reduce_scatter x2 -> x0, waiting for transfers between devices: 122 us -> none  [the longest x1 77.9 us: body(): piece = lax.psum_scatter(partial, 'obs', scatter_dimension=0, tiled=True)]
    all_gather x1 -> x0, waiting for transfers between devices: 47.7 us -> none  [body(): lax.all_gather(alpha_set.reshape(-1, slabs, lanes), 'bel', axis=0, tiled=...]
    pallas_call x2 -> x1, Pallas kernels: 48.1 us -> 85.9 us  [fused(): pl.pallas_call(functools.partial(fused_kernel, plan, names), out_shape=ja...]
    all_gather x1 -> x0, blocking collectives: 31.3 us -> none  [body(): lax.all_gather(piece[beliefs + actions:], 'obs', axis=1, tiled=True)]
    unnamed x12 -> x1, local copies, waits for them, and re-layouts: 11.7 us -> 1.77 us
    reduce_sum x2 -> x0, other arithmetic: 8.03 us -> none  [the longest x1 7.95 us: body(): jnp.sum(transitions.astype(jnp.float32), axis=1)]
  transfers between devices with their start and end apart: 3 -> 0, of which waited for: 3 -> 0; matrix products, arithmetic and copies ran while one was open for 5% -> 0% of each run, Pallas kernels for 0% -> 0%
where the time goes in v2:
time: 89.1 us; the launch traced here: 88.9 us
  Pallas kernels  85.9 us (96%)
  local copies, waits for them, and re-layouts  3.01 us (3%)
    pallas_call x1, Pallas kernels, fused(): pl.pallas_call(functools.partial(fused_kernel, plan, names), out_shape=ja...  85.9 us

profile of v2, /device:TPU:0, one launch (start us, length us, event | category | flops | bytes accessed | tf_op | source)
XLA Modules:
  0.0 88.9 jit_solution(6466028620192651502)
XLA Ops:
  0.0 1.2 %broadcast_in_dim.3.refs_1_ = s32[1,384]{1,0:T(1,128)} reshape(s32[384]{0:T(512)} %refs_0_.1) | data formatting | bytes 3072 | tf_op jit(solution)/shard_map/broadcast_in_dim | solution.py:785
  1.2 85.9 %backup.1 = f32[48,2048]{1,0:T(8,128)} custom-call(s32[384]{0:T(512)} %refs_0_.1, s32[1,384]{1,0:T(1,128)} %broadcast_in_dim.3.refs_1_, f32[16,2048]{1,0:T(8,128)} %refs_2_.1, s32[16,32,384]{2,1,0:T(8,128)} %bitcast.3, bf16[512,2048]{1,0:T(8,128)(2,1)} %refs_4_.1, f32[32,16,2048]{2,1,0:T(8,128)} %refs_5_.1, bf16[4096,2048]{1,0:T(8,128)(2,1)} %bitcast.2), custom_call_target="tpu_custom_call" | custom-call | tf_op jit(solution)/shard_map/backup/pallas_call | solution.py:773
  87.2 1.8 %copy.8 = f32[48,2048]{1,0:T(8,128)} copy(f32[48,2048]{1,0:T(8,128)} %backup.1) | data formatting | bytes 786432

commit v3 on v2

--- a/solution.py
+++ b/solution.py
@@ -133,13 +133,15 @@
 
 def fused_kernel(plan, names, *refs):
     r = types.SimpleNamespace(**dict(zip(names, refs)))
-    ranks, groups, actions, obs_local, rows, cols, beliefs, chunk, width = plan
+    ranks, groups, actions, obs_local, rows, cols, beliefs, parts_of, width = plan
     zs, ys = ranks // 2, groups // 2
     sps = cols // lanes
     slabs = zs * sps
     owned = beliefs // ranks
     half_obs = obs_local // 2
-    chunks = beliefs // chunk
+    chunk, tail = parts_of
+    first_rows = ranks * chunk
+    counts = (ranks, ranks * tail // chunk)
     steps = zs * 2 * cols // width
     share = steps // groups
     parts = r.a_yr.shape[2]
@@ -171,6 +173,15 @@
             device_id_type=MESH,
         )
 
+    def drain_sends(ref, sem):
+        remote(ref, ref, sem, sem, x_peer).wait_send()
+
+    def drain_receives(ref, sem):
+        remote(ref, ref, sem, sem, x_peer).wait_recv()
+
+    def drain_local(ref, sem):
+        pltpu.make_async_copy(ref, ref, sem).wait()
+
     def band(s):
         return pl.ds(pl.multiple_of(s * cols, lanes), cols)
 
@@ -180,22 +191,22 @@
     def half(side):
         return pl.ds(side * half_obs, half_obs)
 
-    own_idx = pltpu.make_async_copy(r.idx, r.idx_in, r.pk_l.at[2 * obs_local])
+    own_idx = pltpu.make_async_copy(r.idx, r.idx_in, r.idx_sem)
     peer_w = [
         pltpu.make_async_copy(
-            r.weights.at[half(c), :, source_band(s, 1 - x)], r.w_src.at[s], r.loc_sem.at[2, s]
+            r.weights.at[half(c), :, source_band(s, 1 - x)], r.w_src.at[s], r.loc_sem.at[s]
         )
         for s in range(zs)
     ]
     own_w = [
         pltpu.make_async_copy(
-            r.weights.at[:, :, source_band(s, x)], r.wraw.at[:, :, band(s)], r.loc_sem.at[0, s]
+            r.weights.at[:, :, source_band(s, x)], r.wraw.at[:, :, band(s)], r.ow_sem
         )
         for s in range(zs)
     ]
     own_a = [
         pltpu.make_async_copy(
-            r.alpha.at[:, source_band(s, x)], r.araw.at[me_b, :, band(s)], r.loc_sem.at[1, s]
+            r.alpha.at[:, source_band(s, x)], r.araw.at[me_b, :, band(s)], r.oa_sem
         )
         for s in range(zs)
     ]
@@ -203,7 +214,7 @@
     for k in range(steps):
         n = lax.rem(me_b * share + k, steps)
         at = pl.ds(pl.multiple_of(n * width, lanes), width)
-        table.append(pltpu.make_async_copy(r.trans.at[:, at], r.tvm.at[n], r.tr_sem.at[k]))
+        table.append(pltpu.make_async_copy(r.trans.at[:, at], r.tvm.at[n], r.tr_sem.at[min(k, share)]))
     for copy in peer_w + [own_idx] + own_w + table[:share] + own_a + table[share:]:
         copy.start()
 
@@ -223,11 +234,8 @@
         return 2 * k + 1 - odd
 
     pieces = [(k, h) for k in range(pairs) for h in range(parts)]
-    sent = []
-
     def launch(copy):
         copy.start()
-        sent.append(copy)
 
     for k, h in pieces:
         for d in range(1, ys):
@@ -235,7 +243,7 @@
                 remote(
                     r.alpha.at[rows_of(h), source_band(near(k), x)],
                     r.araw.at[me_b, rows_of(h), band(near(k))],
-                    r.a_ys.at[d - 1, k, h],
+                    r.a_ys.at[d - 1],
                     r.a_yr.at[d - 1, k, h],
                     y_peer[d],
                 )
@@ -244,8 +252,8 @@
         remote(
             r.alpha.at[:, source_band(s, x)],
             r.araw.at[me_b, :, band(s)],
-            r.a_ps.at[s],
-            r.a_pr.at[s],
+            r.a_ps,
+            r.a_pr,
             core_peer,
         )
         for s in range(zs)
@@ -263,9 +271,9 @@
             r.w_scale_s[s, :, at : at + lanes] = top * (1.0 / code_top)
         w_out.append(
             (
-                remote(r.w_code_s.at[s], r.w_code.at[c, s], r.w_xs.at[0, s], r.w_xr.at[0, s], x_peer),
+                remote(r.w_code_s.at[s], r.w_code.at[c, s], r.w_xs.at[0], r.w_xr.at[0, s], x_peer),
                 remote(
-                    r.w_scale_s.at[s], r.w_scale.at[c, s], r.w_xs.at[1, s], r.w_xr.at[1, s], x_peer
+                    r.w_scale_s.at[s], r.w_scale.at[c, s], r.w_xs.at[1], r.w_xr.at[1, s], x_peer
                 ),
             )
         )
@@ -273,19 +281,16 @@
             launch(copy)
 
     pick_sm = [getattr(r, f"pick_{k}") for k in range(2 * obs_local)]
-    waiting = []
 
     def store_picks(source, first):
         for o in range(obs_local):
-            copy = pltpu.make_async_copy(
-                source.at[pl.ds(o, 1), :], pick_sm[first + o], r.pk_l.at[first + o]
-            )
-            copy.start()
-            waiting.append(copy)
+            pltpu.make_async_copy(
+                source.at[pl.ds(o, 1), :], pick_sm[first + o], r.pk_l.at[first // obs_local]
+            ).start()
 
     def own_picks():
         own_idx.wait()
-        action_row = r.act_row[...]
+        action_row = r.act_row[...].reshape(1, beliefs)
         chosen = jnp.zeros((obs_local, beliefs), jnp.int32)
         for a in range(actions):
             chosen = jnp.where(action_row == a, r.idx_in[a], chosen)
@@ -293,7 +298,7 @@
 
     pick_copy = remote(r.pick_out, r.pick_in, r.pk_s, r.pk_r, x_peer)
     tt_out = [
-        remote(r.tpart, r.tz.at[d - 1], r.tt_zs.at[d - 1], r.tt_zr.at[d - 1], z_peer[d])
+        remote(r.tpart, r.tz.at[d - 1], r.tt_zs, r.tt_zr, z_peer[d])
         for d in range(1, zs)
     ]
     tx_out = remote(r.tx.at[0], r.tx.at[1], r.tt_xs, r.tt_xr, x_peer)
@@ -312,8 +317,10 @@
 
             lax.fori_loop(0, actions, column_total, 0)
 
-    def action_lanes(b, carry):
-        r.actb[pl.ds(b, 1), :] = jnp.full((1, lanes), r.act[b], jnp.int32)
+    def action_lanes(owner, carry):
+        for k in range(owned):
+            at = owner * chunk + k if k < chunk else first_rows + owner * tail + k - chunk
+            r.actb[pl.ds(at, 1), :] = jnp.full((1, lanes), r.act[owner * owned + k], jnp.int32)
         return carry
 
     pad = slabs
@@ -363,12 +370,12 @@
             slot = r.araw.at[member, rows_of(h), band(s)]
             here = (d - 1, k, h)
             if by_z:
-                remote(slot, slot, r.a_zs.at[here], r.a_zr.at[here], next_z).wait_recv()
+                drain_receives(slot, r.a_zr.at[here])
             else:
-                remote(slot, slot, r.a_ys.at[here], r.a_yr.at[here], y_peer[d]).wait_recv()
-                launch(remote(slot, slot, r.a_zs.at[here], r.a_zr.at[here], next_z))
+                drain_receives(slot, r.a_yr.at[here])
+                launch(remote(slot, slot, r.a_zs.at[d - 1], r.a_zr.at[here], next_z))
             at = (d - 1, int(by_z), k, h)
-            forward = remote(slot, slot, r.a_fs.at[at], r.a_fr.at[at], core_peer)
+            forward = remote(slot, slot, r.a_fs.at[d - 1], r.a_fr.at[at], core_peer)
             launch(forward)
             alpha_slab(member, s, h * part_rows, part_rows)
 
@@ -383,7 +390,7 @@
         for k, copy in enumerate(w_out[s]):
             copy.wait_recv()
             held = (r.w_code, r.w_scale)[k].at[c, s]
-            both.append(remote(held, held, r.w_fs.at[k, s], r.w_fr.at[k, s], core_peer))
+            both.append(remote(held, held, r.w_fs.at[k], r.w_fr.at[k, s], core_peer))
             launch(both[-1])
         peer_weight_slab(c, s)
 
@@ -394,6 +401,15 @@
 
         late.append(rest)
 
+    own_picks()
+    pick_copy.start()
+    store_picks(r.pick_out, 0)
+    drain_local(r.wraw, r.ow_sem)
+    for s in range(zs):
+        own_weight_slab(s)
+    drain_local(r.araw.at[me_b], r.oa_sem)
+    for s in range(zs):
+        alpha_slab(me_b, s, 0, rows)
     count = len(pieces)
     for i in range(count + 1):
         ready, late = late, []
@@ -406,30 +422,20 @@
         for rest in ready:
             rest()
         if i == 0:
-            own_picks()
-            for s in range(zs):
-                own_w[s].wait()
-                own_weight_slab(s)
-            pick_copy.start()
-            store_picks(r.pick_out, 0)
-            for s in range(zs):
-                own_a[s].wait()
-                alpha_slab(me_b, s, 0, rows)
-        if i == 1:
             transition_totals()
-            for s in range(zs):
-                a_core[s].wait_recv()
-                alpha_slab(other, s, 0, rows)
             for copy in tt_out:
                 copy.start()
+        if i == 1:
+            drain_receives(r.araw.at[other], r.a_pr)
+            for s in range(zs):
+                alpha_slab(other, s, 0, rows)
         if i == 2:
             pick_copy.wait()
             store_picks(r.pick_in, obs_local)
-            lax.fori_loop(0, beliefs, action_lanes, 0, unroll=8)
     for rest in late:
         rest()
-    for copy in tt_out:
-        copy.wait()
+    drain_sends(r.tz, r.tt_zs)
+    drain_receives(r.tz, r.tt_zr)
     total = r.tpart[...]
     for d in range(1, zs):
         total = total + r.tz[d - 1]
@@ -449,22 +455,22 @@
         remote(
             r.totst.at[pl.ds(pl.multiple_of(z_at[d] * tot_rows, 8), tot_rows)],
             r.totrv.at[d - 1],
-            r.tot_s.at[d - 1],
-            r.tot_r.at[d - 1],
+            r.tot_s,
+            r.tot_r,
             z_peer[d],
         )
         for d in range(1, zs)
     ]
     tall_out = [
         remote(
-            r.tall.at[me_b], r.tall.at[me_b], r.tall_s.at[d - 1], r.tall_r.at[d - 1], b_peer[d]
+            r.tall.at[me_b], r.tall.at[me_b], r.tall_s, r.tall_r, b_peer[d]
         )
         for d in range(1, groups)
     ]
     for copy in tot_out + [tx_out]:
         copy.start()
-    for copy in waiting:
-        copy.wait()
+    drain_local(r.pick_out, r.pk_l.at[0])
+    drain_local(r.pick_in, r.pk_l.at[1])
 
     def share_totals():
         tx_out.wait()
@@ -475,18 +481,24 @@
     def p_copies(q, d):
         here = (q, d - 1)
         return (
-            remote(r.psend.at[here], r.precv.at[here], r.p_s.at[here], r.p_r.at[here], z_peer[d]),
+            remote(r.psend.at[here], r.precv.at[here], r.p_s, r.p_r.at[q], z_peer[d]),
             remote(
-                r.pscale_s.at[here], r.pscale_r.at[here], r.ps_s.at[here], r.ps_r.at[here], z_peer[d]
+                r.pscale_s.at[here], r.pscale_r.at[here], r.ps_s, r.ps_r.at[q], z_peer[d]
             ),
         )
 
     unroll = 4
 
-    def gather_chunk(q):
+    def gather_chunk(q, part):
         def one(i, carry):
+            if part == 0:
+                b0 = q * owned + i * unroll
+            else:
+                row = i * unroll
+                owner = (q - ranks) * (chunk // tail) + lax.div(row, tail)
+                b0 = owner * owned + chunk + lax.rem(row, tail)
             for t in range(unroll):
-                b = q * chunk + i * unroll + t
+                b = b0 + t
                 base = r.act[b] * slabs
                 sums = [None] * 4
                 for p in range(2):
@@ -496,7 +508,7 @@
                         term = row * r.wslab[pl.ds(base + at, slabs), :]
                         k = o % 4
                         sums[k] = term if sums[k] is None else sums[k] + term
-                r.stage[pl.ds(b, slabs, stride=beliefs), :] = (sums[0] + sums[1]) + (
+                r.stage[pl.ds(q * chunk + i * unroll + t, slabs, stride=beliefs), :] = (sums[0] + sums[1]) + (
                     sums[2] + sums[3]
                 )
             return carry
@@ -513,13 +525,21 @@
                 copy.start()
 
     def prepare():
-        for copy in tot_out + tall_out:
-            copy.wait()
+        drain_sends(r.totrv, r.tot_s)
+        drain_receives(r.totrv, r.tot_r)
+        drain_sends(r.tall.at[pl.ds(0, groups - 1)], r.tall_s)
+        drain_receives(r.tall.at[pl.ds(0, groups - 1)], r.tall_r)
         totals = r.totst[pl.ds(pl.multiple_of(z * tot_rows, 8), tot_rows), :]
         for d in range(1, zs):
             totals = totals + r.totrv[d - 1]
         r.tsum[...] = totals
-        own_act = r.actb[pl.ds(pl.multiple_of(me_o * owned, 8), owned), :]
+        own_act = jnp.concatenate(
+            [
+                r.actb[pl.ds(pl.multiple_of(me_o * chunk, 8), chunk), :],
+                r.actb[pl.ds(pl.multiple_of(first_rows + me_o * tail, 8), tail), :],
+            ],
+            axis=0,
+        )
         per_member = share * width // lanes
 
         for member in range(groups):
@@ -535,11 +555,13 @@
                 r.rsel[:, to] = reward
                 r.tsel[:, to] = discount / scale
 
-    def absorb(q):
-        for d in range(1, zs):
-            for copy in p_copies(q, d):
-                copy.wait()
+    def absorb(q, part):
+        drain_receives(r.precv.at[q], r.p_r.at[q])
+        drain_receives(r.pscale_r.at[q], r.ps_r.at[q])
         b0 = pl.multiple_of(q * chunk, 16)
+        into = (r.xbig0, r.xbig1)[part]
+        at_row = pl.multiple_of(q * chunk - part * first_rows, 16)
+        at_low = pl.multiple_of(at_row + into.shape[0] // 2, 16)
         act = r.actb[pl.ds(b0, chunk), :]
         for h in range(sps):
             first = (z * sps + h) * beliefs + q * chunk
@@ -556,15 +578,13 @@
             for a in range(actions):
                 at = slice(a * cols + h * lanes, a * cols + (h + 1) * lanes)
                 hit = act == a
-                r.xbig[pl.ds(b0, chunk), at] = jnp.where(hit, high, 0.0).astype(jnp.bfloat16)
-                r.xbig[pl.ds(pl.multiple_of(beliefs + b0, 16), chunk), at] = jnp.where(
-                    hit, low, 0.0
-                ).astype(jnp.bfloat16)
-
-    behind = min(3, chunks - 1)
-
-    def gather_step(q, carry):
-        gather_chunk(q)
+                into[pl.ds(at_row, chunk), at] = jnp.where(hit, high, 0.0).astype(jnp.bfloat16)
+                into[pl.ds(at_low, chunk), at] = jnp.where(hit, low, 0.0).astype(jnp.bfloat16)
+
+    behind = 3
+
+    def gather_first(q, carry):
+        gather_chunk(q, 0)
 
         @pl.when(q == 0)
         def _():
@@ -576,93 +596,158 @@
 
         @pl.when(q >= behind)
         def _():
-            absorb(q - behind)
+            absorb(q - behind, 0)
 
         return carry
 
-    lax.fori_loop(0, chunks, gather_step, 0)
-
-    def absorb_step(q, carry):
-        absorb(q)
+    def gather_last(j, carry):
+        gather_chunk(ranks + j, 1)
+
+        @pl.when(j < behind)
+        def _():
+            absorb(ranks - behind + j, 0)
+
         return carry
 
-    lax.fori_loop(chunks - behind, chunks, absorb_step, 0)
-    for copy in table[share:]:
-        copy.wait()
-
-    def x_copies(n):
+    lax.fori_loop(0, ranks, action_lanes, 0)
+    lax.fori_loop(0, counts[0], gather_first, 0)
+    lax.fori_loop(0, counts[1], gather_last, 0)
+    drain_local(r.tvm.at[pl.ds(0, steps - share)], r.tr_sem.at[share])
+
+    sizes = (chunk, tail)
+    sets = [
+        types.SimpleNamespace(
+            **{name: getattr(r, name + str(part)) for name in part_names}, rows=sizes[part]
+        )
+        for part in range(2)
+    ]
+
+    def x_copies(part, n):
+        t, here = sets[part], (part, n)
         return (
-            remote(r.xsend.at[n], r.xrecv.at[n], r.x_s.at[n], r.x_r.at[n], x_peer),
-            remote(r.xscale_s.at[n], r.xscale_r.at[n], r.xs_s.at[n], r.xs_r.at[n], x_peer),
-        )
-
-    def z_copies(n, d):
-        here = (n, d - 1)
+            remote(t.xsend.at[n], t.xrecv.at[n], r.x_s.at[part], r.x_r.at[here], x_peer),
+            remote(t.xscale_s.at[n], t.xscale_r.at[n], r.xs_s.at[part], r.xs_r.at[here], x_peer),
+        )
+
+    def z_copies(part, n, d):
+        t, here, k = sets[part], (part, n), (n, d - 1)
         return (
-            remote(r.zsend.at[here], r.zrecv.at[here], r.z_s.at[here], r.z_r.at[here], z_peer[d]),
-            remote(r.zscale_s.at[here], r.zscale_r.at[here], r.zs_s.at[here], r.zs_r.at[here], z_peer[d]),
-        )
-
-    def owner_rows(zt, side):
-        return pl.ds(pl.multiple_of((2 * zt + side) * owned, 8), owned)
-
-    def to_pair(n):
-        sides = [r.outp[n, owner_rows(s, 1 - x), :] for s in range(zs)]
-        top = column_top(sides)
+            remote(t.zsend.at[k], t.zrecv.at[k], r.z_s.at[part], r.z_r.at[here], z_peer[d]),
+            remote(
+                t.zscale_s.at[k], t.zscale_r.at[k], r.zs_s.at[part], r.zs_r.at[here], z_peer[d]
+            ),
+        )
+
+    def product(part, n):
+        t = sets[part]
+        both = jnp.dot(t.xbig[...], r.tvm[n], preferred_element_type=jnp.float32)
+        count = both.shape[0] // 2
+        t.outp[n] = both[:count] + both[count:]
+        owner = [
+            t.outp[n, pl.ds(pl.multiple_of((2 * s + 1 - x) * t.rows, 8), t.rows), :]
+            for s in range(zs)
+        ]
+        top = column_top(owner)
         for s in range(zs):
-            r.xsend[n, s * owned : (s + 1) * owned, :] = encode(sides[s], top)
-        r.xscale_s[n] = top * (1.0 / code_top)
-        for copy in x_copies(n):
+            t.xsend[n, s * t.rows : (s + 1) * t.rows, :] = encode(owner[s], top)
+        t.xscale_s[n] = top * (1.0 / code_top)
+        for copy in x_copies(part, n):
             copy.start()
 
-    def to_owners(n):
-        for copy in x_copies(n):
-            copy.wait()
-        scale = r.xscale_r[n]
+    def to_owners(part, n):
+        t = sets[part]
+        for copy in x_copies(part, n):
+            copy.wait_recv()
+        scale = t.xscale_r[n]
         for s in range(zs):
-            part = slice(s * owned, (s + 1) * owned)
-            r.ysum[n, part, :] = r.outp[n, owner_rows(s, x), :] + decode(r.xrecv[n, part, :], scale)
+            at = slice(s * t.rows, (s + 1) * t.rows)
+            kept = t.outp[n, pl.ds(pl.multiple_of((2 * s + x) * t.rows, 8), t.rows), :]
+            t.ysum[n, at, :] = kept + decode(t.xrecv[n, at, :], scale)
         for d in range(1, zs):
-            value = r.ysum[n, pl.ds(pl.multiple_of(z_at[d] * owned, 8), owned), :]
+            value = t.ysum[n, pl.ds(pl.multiple_of(z_at[d] * t.rows, 8), t.rows), :]
             top = column_top([value])
-            r.zsend[n, d - 1] = encode(value, top)
-            r.zscale_s[n, d - 1] = top * (1.0 / code_top)
-            for copy in z_copies(n, d):
+            t.zsend[n, d - 1] = encode(value, top)
+            t.zscale_s[n, d - 1] = top * (1.0 / code_top)
+            for copy in z_copies(part, n, d):
                 copy.start()
 
-    def finish(n):
-        value = r.ysum[n, pl.ds(pl.multiple_of(z * owned, 8), owned), :]
+    def finish(part, n):
+        t = sets[part]
+        value = t.ysum[n, pl.ds(pl.multiple_of(z * t.rows, 8), t.rows), :]
+        drain_receives(t.zrecv.at[n], r.z_r.at[part, n])
+        drain_receives(t.zscale_r.at[n], r.zs_r.at[part, n])
         for d in range(1, zs):
-            for copy in z_copies(n, d):
-                copy.wait()
-            value = value + decode(r.zrecv[n, d - 1], r.zscale_r[n, d - 1])
+            value = value + decode(t.zrecv[n, d - 1], t.zscale_r[n, d - 1])
         at = pl.ds(pl.multiple_of(n * width, width), width)
-        r.out[:, at] = r.rsel[:, at] + value * r.tsel[:, at]
-
-    pair_lag, lag = min(2, steps), min(5, steps)
-
-    def step(n, carry):
-        both = jnp.dot(r.xbig[...], r.tvm[n], preferred_element_type=jnp.float32)
-        r.outp[n] = both[:beliefs] + both[beliefs:]
-        to_pair(n)
-
-        @pl.when(n >= pair_lag)
-        def _():
-            to_owners(n - pair_lag)
+        to = slice(part * chunk, part * chunk + t.rows)
+        r.out[to, at] = r.rsel[to, at] + value * r.tsel[to, at]
+
+    lag = min(3, steps)
+
+    def first_step(n, carry):
+        product(0, n)
 
         @pl.when(n >= lag)
         def _():
-            finish(n - lag)
+            to_owners(0, n - lag)
+
+        @pl.when(n >= steps - counts[1])
+        def _():
+            absorb(ranks + n - (steps - counts[1]), 1)
 
         return carry
 
-    lax.fori_loop(0, steps, step, 0)
-    for n in range(steps - pair_lag, steps):
-        to_owners(n)
+    def last_step(n, carry):
+        product(1, n)
+
+        @pl.when(n < lag)
+        def _():
+            to_owners(0, n + steps - lag)
+
+        @pl.when(n >= lag)
+        def _():
+            to_owners(1, n - lag)
+
+        finish(0, n)
+        return carry
+
+    lax.fori_loop(0, steps, first_step, 0)
+    lax.fori_loop(0, steps, last_step, 0)
     for n in range(steps - lag, steps):
-        finish(n)
-    for copy in sent:
-        copy.wait_send()
+        to_owners(1, n)
+    for n in range(steps):
+        finish(1, n)
+    for part, t in enumerate(sets):
+        drain_sends(t.xsend, r.x_s.at[part])
+        drain_sends(t.xscale_s, r.xs_s.at[part])
+        drain_sends(t.zsend, r.z_s.at[part])
+        drain_sends(t.zscale_s, r.zs_s.at[part])
+    drain_sends(r.psend, r.p_s)
+    drain_sends(r.pscale_s, r.ps_s)
+    drain_sends(r.w_code_s, r.w_xs.at[0])
+    drain_sends(r.w_scale_s, r.w_xs.at[1])
+    drain_sends(r.w_code.at[0], r.w_fs.at[0])
+    drain_sends(r.w_scale.at[0], r.w_fs.at[1])
+    drain_sends(r.araw.at[0], r.a_ps)
+    for d in range(1, ys):
+        drain_sends(r.araw.at[0, :, pl.ds(0, pairs * cols)], r.a_ys.at[d - 1])
+        drain_sends(r.araw.at[0, :, pl.ds(0, pairs * cols)], r.a_zs.at[d - 1])
+        drain_sends(r.araw.at[0], r.a_fs.at[d - 1])
+
+
+part_names = (
+    "xbig",
+    "outp",
+    "ysum",
+    "xsend",
+    "xrecv",
+    "xscale_s",
+    "xscale_r",
+    "zsend",
+    "zrecv",
+    "zscale_s",
+    "zscale_r",
+)
 
 
 def fused(alpha_set, transitions, obs_weights, rewards, chosen_idx, chosen_action, groups):
@@ -677,14 +762,15 @@
     slabs = zs * sps
     owned = beliefs // ranks
     half_obs = obs_local // 2
-    chunks = 8
-    chunk = beliefs // chunks
+    tail = 16
+    chunk = owned - tail
+    chunks = ranks + ranks * tail // chunk
     width = 256
     steps = states // width
     xc = zs * cols
     shared = states // groups
     outer, parts, pairs = max(ys - 1, 1), 2, zs // 2
-    plan = (ranks, groups, actions, obs_local, rows, cols, beliefs, chunk, width)
+    plan = (ranks, groups, actions, obs_local, rows, cols, beliefs, (chunk, tail), width)
     f32, bf16, i16, i32 = jnp.float32, jnp.bfloat16, jnp.int16, jnp.int32
     vmem, dma = pltpu.VMEM, pltpu.SemaphoreType.DMA
     scratch = dict(
@@ -710,17 +796,6 @@
         precv=vmem((chunks, zs - 1, sps, chunk, lanes), i16),
         pscale_s=vmem((chunks, zs - 1, sps, lanes), f32),
         pscale_r=vmem((chunks, zs - 1, sps, lanes), f32),
-        xbig=vmem((2 * beliefs, actions * cols), bf16),
-        outp=vmem((steps, beliefs, width), f32),
-        ysum=vmem((steps, zs * owned, width), f32),
-        xsend=vmem((steps, zs * owned, width), i16),
-        xrecv=vmem((steps, zs * owned, width), i16),
-        xscale_s=vmem((steps, 1, width), f32),
-        xscale_r=vmem((steps, 1, width), f32),
-        zsend=vmem((steps, zs - 1, owned, width), i16),
-        zrecv=vmem((steps, zs - 1, owned, width), i16),
-        zscale_s=vmem((steps, zs - 1, 1, width), f32),
-        zscale_r=vmem((steps, zs - 1, 1, width), f32),
         tpart=vmem((actions, shared), f32),
         tz=vmem((zs - 1, actions, shared), f32),
         tx=vmem((2, actions, shared), f32),
@@ -728,44 +803,62 @@
         rsel=vmem((owned, states), f32),
         tsel=vmem((owned, states), f32),
         **{f"pick_{k}": pltpu.SMEM((1, beliefs), i32) for k in range(2 * obs_local)},
-        pk_l=dma((2 * obs_local + 1,)),
-        loc_sem=dma((3, zs)),
-        tr_sem=dma((steps,)),
-        a_ys=dma((outer, pairs, parts)),
+        pk_l=dma((2,)),
+        idx_sem=dma(()),
+        ow_sem=dma(()),
+        oa_sem=dma(()),
+        loc_sem=dma((zs,)),
+        tr_sem=dma((steps // groups + 1,)),
+        a_ys=dma((outer,)),
         a_yr=dma((outer, pairs, parts)),
-        a_zs=dma((outer, pairs, parts)),
+        a_zs=dma((outer,)),
         a_zr=dma((outer, pairs, parts)),
-        a_fs=dma((outer, 2, pairs, parts)),
+        a_fs=dma((outer,)),
         a_fr=dma((outer, 2, pairs, parts)),
-        a_ps=dma((zs,)),
-        a_pr=dma((zs,)),
-        w_xs=dma((2, zs)),
+        a_ps=dma(()),
+        a_pr=dma(()),
+        w_xs=dma((2,)),
         w_xr=dma((2, zs)),
-        w_fs=dma((2, zs)),
+        w_fs=dma((2,)),
         w_fr=dma((2, zs)),
         pk_s=dma(()),
         pk_r=dma(()),
-        tt_zs=dma((zs - 1,)),
-        tt_zr=dma((zs - 1,)),
+        tt_zs=dma(()),
+        tt_zr=dma(()),
         tt_xs=dma(()),
         tt_xr=dma(()),
-        tall_s=dma((groups - 1,)),
-        tall_r=dma((groups - 1,)),
-        tot_s=dma((zs - 1,)),
-        tot_r=dma((zs - 1,)),
-        p_s=dma((chunks, zs - 1)),
-        p_r=dma((chunks, zs - 1)),
-        ps_s=dma((chunks, zs - 1)),
-        ps_r=dma((chunks, zs - 1)),
-        x_s=dma((steps,)),
-        x_r=dma((steps,)),
-        xs_s=dma((steps,)),
-        xs_r=dma((steps,)),
-        z_s=dma((steps, zs - 1)),
-        z_r=dma((steps, zs - 1)),
-        zs_s=dma((steps, zs - 1)),
-        zs_r=dma((steps, zs - 1)),
+        tall_s=dma(()),
+        tall_r=dma(()),
+        tot_s=dma(()),
+        tot_r=dma(()),
+        p_s=dma(()),
+        p_r=dma((chunks,)),
+        ps_s=dma(()),
+        ps_r=dma((chunks,)),
+        x_s=dma((2,)),
+        x_r=dma((2, steps)),
+        xs_s=dma((2,)),
+        xs_r=dma((2, steps)),
+        z_s=dma((2,)),
+        z_r=dma((2, steps)),
+        zs_s=dma((2,)),
+        zs_r=dma((2, steps)),
     )
+    for part, count in enumerate((chunk, tail)):
+        shapes = (
+            vmem((2 * ranks * count, actions * cols), bf16),
+            vmem((steps, ranks * count, width), f32),
+            vmem((steps, zs * count, width), f32),
+            vmem((steps, zs * count, width), i16),
+            vmem((steps, zs * count, width), i16),
+            vmem((steps, 1, width), f32),
+            vmem((steps, 1, width), f32),
+            vmem((steps, zs - 1, count, width), i16),
+            vmem((steps, zs - 1, count, width), i16),
+            vmem((steps, zs - 1, 1, width), f32),
+            vmem((steps, zs - 1, 1, width), f32),
+        )
+        scratch.update(zip([name + str(part) for name in part_names], shapes))
     hbm = pl.BlockSpec(memory_space=pl.ANY)
     smem = pl.BlockSpec(memory_space=pltpu.SMEM)
     local = pl.BlockSpec(memory_space=pltpu.VMEM)
@@ -782,7 +875,7 @@
         name="backup",
     )(
         chosen_action,
-        chosen_action[None, :],
+        chosen_action,
         rewards,
         chosen_idx.transpose(1, 2, 0),
         alpha_set,
@@ -804,7 +897,10 @@
         and obs_local % 2 == 0
         and alpha_set.shape[0] % 64 == 0
         and beliefs % (16 * ranks) == 0
-        and beliefs % 128 == 0
+        and beliefs > 16 * ranks
+        and ranks * 16 % (beliefs // ranks - 16) == 0
+        and ranks * 16 // (beliefs // ranks - 16) <= states // 256
+        and ranks * 16 // (beliefs // ranks - 16) >= 3
     )
 
 

time: 89.1 us -> 84.2 us (0.945)
  Pallas kernels: 85.9 us -> 82.2 us
  local copies, waits for them, and re-layouts: 3.01 us -> 1.77 us
    pallas_call x1, Pallas kernels: 85.9 us -> 82.2 us  [fused(): pl.pallas_call(functools.partial(fused_kernel, plan, names), out_shape=ja...]
    broadcast_in_dim x1 -> x0, local copies, waits for them, and re-layouts: 1.24 us -> none  [fused(): chosen_action[None, :]]
where the time goes in v3:
time: 84.2 us; the launch traced here: 84 us
  Pallas kernels  82.2 us (98%)
  local copies, waits for them, and re-layouts  1.77 us (2%)
    pallas_call x1, Pallas kernels, fused(): pl.pallas_call(functools.partial(fused_kernel, plan, names), out_shape=ja...  82.2 us
    unnamed x1, local copies, waits for them, and re-layouts  1.77 us

profile of v3, /device:TPU:0, one launch (start us, length us, event | category | flops | bytes accessed | tf_op | source)
XLA Modules:
  0.0 84.0 jit_solution(12545037400228067937)
XLA Ops:
  0.0 82.2 %backup.1 = f32[48,2048]{1,0:T(8,128)} custom-call(s32[384]{0:T(512)} %refs_1_.1, s32[384]{0:T(512)} %refs_1_.1, f32[16,2048]{1,0:T(8,128)} %refs_2_.1, s32[16,32,384]{2,1,0:T(8,128)} %bitcast.3, bf16[512,2048]{1,0:T(8,128)(2,1)} %refs_4_.1, f32[32,16,2048]{2,1,0:T(8,128)} %refs_5_.1, bf16[4096,2048]{1,0:T(8,128)(2,1)} %bitcast.2), custom_call_target="tpu_custom_call" | custom-call | tf_op jit(solution)/shard_map/backup/pallas_call | solution.py:866
  82.2 1.8 %copy.8 = f32[48,2048]{1,0:T(8,128)} copy(f32[48,2048]{1,0:T(8,128)} %backup.1) | data formatting | bytes 786432

commit v4 on v3

--- a/solution.py
+++ b/solution.py
@@ -191,6 +191,11 @@
     def half(side):
         return pl.ds(side * half_obs, half_obs)
 
+    small = [
+        pltpu.make_async_copy(r.act_hbm, r.act, r.small_sem.at[0]),
+        pltpu.make_async_copy(r.act_hbm, r.act_row, r.small_sem.at[1]),
+        pltpu.make_async_copy(r.rew_hbm, r.rew, r.small_sem.at[2]),
+    ]
     own_idx = pltpu.make_async_copy(r.idx, r.idx_in, r.idx_sem)
     peer_w = [
         pltpu.make_async_copy(
@@ -215,7 +220,7 @@
         n = lax.rem(me_b * share + k, steps)
         at = pl.ds(pl.multiple_of(n * width, lanes), width)
         table.append(pltpu.make_async_copy(r.trans.at[:, at], r.tvm.at[n], r.tr_sem.at[min(k, share)]))
-    for copy in peer_w + [own_idx] + own_w + table[:share] + own_a + table[share:]:
+    for copy in peer_w + [own_idx] + small + own_w + table[:share] + own_a + table[share:]:
         copy.start()
 
     peers = [x_peer] + z_peer[1:] + b_peer[1:]
@@ -289,7 +294,8 @@
             ).start()
 
     def own_picks():
-        own_idx.wait()
+        for copy in small + [own_idx]:
+            copy.wait()
         action_row = r.act_row[...].reshape(1, beliefs)
         chosen = jnp.zeros((obs_local, beliefs), jnp.int32)
         for a in range(actions):
@@ -410,6 +416,7 @@
     drain_local(r.araw.at[me_b], r.oa_sem)
     for s in range(zs):
         alpha_slab(me_b, s, 0, rows)
+    lax.fori_loop(0, ranks, action_lanes, 0)
     count = len(pieces)
     for i in range(count + 1):
         ready, late = late, []
@@ -527,12 +534,14 @@
     def prepare():
         drain_sends(r.totrv, r.tot_s)
         drain_receives(r.totrv, r.tot_r)
-        drain_sends(r.tall.at[pl.ds(0, groups - 1)], r.tall_s)
-        drain_receives(r.tall.at[pl.ds(0, groups - 1)], r.tall_r)
         totals = r.totst[pl.ds(pl.multiple_of(z * tot_rows, 8), tot_rows), :]
         for d in range(1, zs):
             totals = totals + r.totrv[d - 1]
         r.tsum[...] = totals
+
+    def own_rows():
+        drain_sends(r.tall.at[pl.ds(0, groups - 1)], r.tall_s)
+        drain_receives(r.tall.at[pl.ds(0, groups - 1)], r.tall_r)
         own_act = jnp.concatenate(
             [
                 r.actb[pl.ds(pl.multiple_of(me_o * chunk, 8), chunk), :],
@@ -607,9 +616,12 @@
         def _():
             absorb(ranks - behind + j, 0)
 
+        @pl.when(j == counts[1] - 1)
+        def _():
+            own_rows()
+
         return carry
 
-    lax.fori_loop(0, ranks, action_lanes, 0)
     lax.fori_loop(0, counts[0], gather_first, 0)
     lax.fori_loop(0, counts[1], gather_last, 0)
     drain_local(r.tvm.at[pl.ds(0, steps - share)], r.tr_sem.at[share])
@@ -774,6 +786,10 @@
     f32, bf16, i16, i32 = jnp.float32, jnp.bfloat16, jnp.int16, jnp.int32
     vmem, dma = pltpu.VMEM, pltpu.SemaphoreType.DMA
     scratch = dict(
+        act=pltpu.SMEM((beliefs,), i32),
+        act_row=vmem((beliefs,), i32),
+        rew=vmem((actions, states), f32),
+        small_sem=dma((3,)),
         idx_in=vmem((actions, obs_local, beliefs), i32),
         araw=vmem((groups, rows, xc), bf16),
         aslab=vmem((groups * rows * slabs, lanes), f32),
@@ -860,13 +876,12 @@
         )
         scratch.update(zip([name + str(part) for name in part_names], shapes))
     hbm = pl.BlockSpec(memory_space=pl.ANY)
-    smem = pl.BlockSpec(memory_space=pltpu.SMEM)
     local = pl.BlockSpec(memory_space=pltpu.VMEM)
-    names = ("act", "act_row", "rew", "idx", "alpha", "weights", "trans", "out", *scratch)
+    names = ("act_hbm", "rew_hbm", "idx", "alpha", "weights", "trans", "out", *scratch)
     return pl.pallas_call(
         functools.partial(fused_kernel, plan, names),
         out_shape=jax.ShapeDtypeStruct((owned, states), f32),
-        in_specs=[smem, local, local, hbm, hbm, hbm, hbm],
+        in_specs=[hbm] * 6,
         out_specs=local,
         scratch_shapes=list(scratch.values()),
         compiler_params=pltpu.CompilerParams(
@@ -874,7 +889,6 @@
         ),
         name="backup",
     )(
-        chosen_action,
         chosen_action,
         rewards,
         chosen_idx.transpose(1, 2, 0),

time: 84.2 us -> 82.9 us (0.985)
  Pallas kernels: 82.2 us -> 80.9 us
    pallas_call x1, Pallas kernels: 82.2 us -> 80.9 us  [fused(): pl.pallas_call(functools.partial(fused_kernel, plan, names), out_shape=ja...]
where the time goes in v4:
time: 82.9 us; the launch traced here: 82.7 us
  Pallas kernels  80.9 us (98%)
  local copies, waits for them, and re-layouts  1.77 us (2%)
    pallas_call x1, Pallas kernels, fused(): pl.pallas_call(functools.partial(fused_kernel, plan, names), out_shape=ja...  80.9 us
    unnamed x1, local copies, waits for them, and re-layouts  1.77 us

profile of v4, /device:TPU:0, one launch (start us, length us, event | category | flops | bytes accessed | tf_op | source)
XLA Modules:
  0.0 82.7 jit_solution(7776860882973141698)
XLA Ops:
  0.0 80.9 %backup.1 = f32[48,2048]{1,0:T(8,128)} custom-call(s32[384]{0:T(512)} %refs_0_.1, f32[16,2048]{1,0:T(8,128)} %refs_1_.1, s32[16,32,384]{2,1,0:T(8,128)} %bitcast.3, bf16[512,2048]{1,0:T(8,128)(2,1)} %refs_3_.1, f32[32,16,2048]{2,1,0:T(8,128)} %refs_4_.1, bf16[4096,2048]{1,0:T(8,128)(2,1)} %bitcast.2), custom_call_target="tpu_custom_call" | custom-call | tf_op jit(solution)/shard_map/backup/pallas_call | solution.py:881
  80.9 1.8 %copy.8 = f32[48,2048]{1,0:T(8,128)} copy(f32[48,2048]{1,0:T(8,128)} %backup.1) | data formatting | bytes 786432
